TPU v7x, 256 devices: a whole 4x4x8 slice. The times are simulated.
256 devices in a mesh: slab: 32 (over z, y), energy: 8 (over x, core).
Axes of the slice: x: 4, y: 4, z: 8, core: 2. Of those that a mesh axis runs over, the one named last changes fastest.
Arguments:
- green: bfloat16 [8, 32, 3, 2, 384, 384], P('energy', 'slab'), may hold values from -0.3125 to 0.3125
- sigma: bfloat16 [8, 32, 3, 2, 384, 384], P('energy', 'slab'), may hold values from -4 to 4
- phonon: bfloat16 [8, 32, 2, 384, 384], P('energy', 'slab'), may hold values from -4 to 4
- pair_off: int32 [32, 3], replicated, may hold values from -2 to 2, as said below
- pair_count: int32 [32], replicated, may hold values from 1 to 3, as said below
- pair_range: int32 [32, 3], replicated, may hold values from 96 to 384, as said below
Outputs:
- lesser: float32 [8, 32, 2, 384, 384], P('energy', 'slab')
Inputs may be any that keep to these rules, and one draw needn't show every extreme that they name: The partner slab k + pair_off[k, q] lies inside the grid. `pair_count`: some slab has 3 live slots. `pair_range`: a multiple of 96; some pair couples all 384 orbitals.
All inputs are finite; a program needn't handle non-finite values.
Results may differ from a plain program's by a relative error of at most 0.0035.
Values may be sent and summed in bfloat16 or wider, within the bound.
No kernel may reach another device: no remote copies, remote signals or barrier semaphores. Data moves between devices by JAX's collectives and lax.ppermute only.
A program may use at most 64 MiB of HBM per device.

v0:
```python
import jax
import jax.numpy as jnp
from jax import lax
from jax.sharding import PartitionSpec as P


def from_behind(value, axis, steps):
    count = lax.axis_size(axis)
    leading, last = (max(0, -steps), min(count, count - steps))
    return lax.ppermute(value, axis, [(source, source + steps) for source in range(leading, last)])


def extended_2(block, sides, width):
    for axis, dim in sides:
        count = lax.axis_size(axis)
        forward = [(i, i + 1) for i in range(count - 1)]
        backward = [(target, source) for source, target in forward]
        low = lax.ppermute(
            lax.slice_in_dim(block, block.shape[dim] - width, None, axis=dim), axis, forward
        )
        high = lax.ppermute(lax.slice_in_dim(block, 0, width, axis=dim), axis, backward)
        block = jnp.concatenate([low, block, high], axis=dim)
    return block


def conj_sum(source, chosen):
    layout = (((0, 2), (0, 2)), ((), ()))

    def pair_dot(left, right):
        return lax.dot_general(left, right, layout, preferred_element_type=jnp.float32)

    real = pair_dot(source[:, 0], chosen[:, 0]) + pair_dot(source[:, 1], chosen[:, 1])
    imag = pair_dot(source[:, 1], chosen[:, 0]) - pair_dot(source[:, 0], chosen[:, 1])
    return (real, imag)


def complex_times(left, real, imag):
    first = jnp.dot(left[0], real, preferred_element_type=jnp.float32) - jnp.dot(
        left[1], imag, preferred_element_type=jnp.float32
    )
    second = jnp.dot(left[0], imag, preferred_element_type=jnp.float32) + jnp.dot(
        left[1], real, preferred_element_type=jnp.float32
    )
    return jnp.stack([first, second])


def slab_term(green_row, source, other, row_slab, diag_at, pair_off, pair_count):
    slab_total = pair_off.shape[0]
    slots = pair_off.shape[1]
    clipped = jnp.clip(other, 0, slab_total - 1)
    offsets = lax.dynamic_index_in_dim(pair_off, clipped, 0, keepdims=False)
    count = lax.dynamic_index_in_dim(pair_count, clipped, 0, keepdims=False)
    place = clipped + offsets - row_slab + 1
    slot_ids = jnp.arange(slots, dtype=jnp.int32)
    usable = (place >= 0) & (place <= 2) & (slot_ids < count)
    pick = jnp.concatenate([jnp.clip(place, 0, 2), jnp.full((1,), diag_at, jnp.int32)])
    keep = jnp.concatenate([usable, jnp.ones((1,), bool)]).astype(jnp.bfloat16)
    chosen = jnp.take(green_row, pick, axis=0) * keep[:, None, None, None]
    real, imag = conj_sum(source, chosen)
    return complex_times(green_row[diag_at], real.astype(jnp.bfloat16), imag.astype(jnp.bfloat16))


def body(green, sigma, phonon, pair_off, pair_count, pair_range):
    slab_count = green.shape[1]
    width = green.shape[-1]
    first_slab = lax.axis_index("slab") * slab_count
    sides = [from_behind(phonon, "energy", shift_by) for shift_by in (1, -1)]
    phonon_mix = (0.5 * (sides[0].astype(jnp.float32) + sides[1].astype(jnp.float32))).astype(
        jnp.bfloat16
    )
    local_range = lax.dynamic_slice_in_dim(pair_range, first_slab, slab_count, 0)
    positions = jnp.arange(width, dtype=jnp.int32)
    inside = positions[None, None, :] < local_range[:, :, None]
    square = inside[:, :, :, None] & inside[:, :, None, :]
    masked = jnp.where(square[:, :, None], sigma[0], jnp.zeros((), jnp.bfloat16))
    stacked = jnp.concatenate([masked, phonon_mix[0][:, None]], axis=1)
    extended = extended_2(stacked, (("slab", 0),), 1)
    row_slab = first_slab + 0
    green_row = green[0, 0]
    running = jnp.zeros((2, width, width), jnp.float32)
    for delta in (-1, 0, 1):
        running = running + slab_term(
            green_row,
            extended[1 + delta],
            row_slab + delta,
            row_slab,
            delta + 1,
            pair_off,
            pair_count,
        )
    results = [running]
    return jnp.stack(results)[None]


def solution(mesh):
    in_specs = (
        P("energy", "slab", None, None, None, None),
        P("energy", "slab", None, None, None, None),
        P("energy", "slab", None, None, None),
        P(),
        P(),
        P(),
    )
    out_specs = P("energy", "slab", None, None, None)
    return jax.shard_map(body, mesh=mesh, in_specs=in_specs, out_specs=out_specs, check_vma=False)
```

profile of v0, /device:TPU:130, one launch (start us, length us, event | category | flops | bytes accessed | tf_op | source)
XLA Modules:
  0.0 112.8 jit_solution(13357998503600026632)
XLA Ops:
  0.0 2.0 %collective-permute-start = (bf16[1,1,2,384,384]{4,3,1,2,0:T(8,128)(2,1)}, bf16[1,1,2,384,384]{4,3,1,2,0:T(8,128)(2,1)}, u32[]{:S(2)}, u32[]{:S(2)}) collective-permute-start(bf16[1,1,2,384,384]{4,3,1,2,0:T(8,128)(2,1)} %bitcast.181), channel_id=1, source_target_pairs={{0,1},{1,2},{2,3},{3,4},{4,5},{5,6},{6,7},{8,9},{9,10},{10,11},{11... | collective-permute-start | bytes 1769480 | tf_op jit(solution)/shard_map/ppermute | solution.py:10
  2.1 3.6 %collective-permute-start.1 = (bf16[1,1,2,384,384]{4,3,1,2,0:T(8,128)(2,1)}, bf16[1,1,2,384,384]{4,3,1,2,0:T(8,128)(2,1)}, u32[]{:S(2)}, u32[]{:S(2)}) collective-permute-start(bf16[1,1,2,384,384]{4,3,1,2,0:T(8,128)(2,1)} %bitcast.182), channel_id=1, source_target_pairs={{1,0},{2,1},{3,2},{4,3},{5,4},{6,5},{7,6},{9,8},{10,9},{11,10},{12... | collective-permute-start | bytes 1769480 | tf_op jit(solution)/shard_map/ppermute | solution.py:10
  5.7 1.5 %and_reduce_fusion = (pred[3]{0:T(512)(128)(4,1)S(1)}, pred[3]{0:T(512)(128)(4,1)S(1)}, pred[3]{0:T(512)(128)(4,1)}) fusion(s32[]{:T(128)S(6)} %axis_index.15, s32[32,3]{0,1:T(4,128)} %param.11, s32[]{:T(128)S(6)} %min.39, s32[]{:T(128)S(6)} %min.36, s32[]{:T(128)S(6)} %min.32), kind=kLoop, calls=%fused_computation.116 | loop fusion | flops 54 | bytes 3629 | tf_op jit(solution)/shard_map/and | solution.py:55
  7.2 1.0 clamp_reduce_fusion
  8.2 1.4 %fusion.56 = (s32[1]{0:T(128)}, s32[1]{0:T(128)}, s32[1]{0:T(128)}) fusion(s32[32]{0:T(128)} %param.12, s32[]{:T(128)S(6)} %min.39, s32[]{:T(128)S(6)} %min.32, s32[]{:T(128)S(6)} %min.36), kind=kLoop, calls=%fused_computation.123 | loop fusion | bytes 36 | tf_op jit(solution)/shard_map/jit(dynamic_index_in_dim)/dynamic_slice | solution.py:52
  10.6 1.0 broadcast_and_fusion
  11.8 1.7 %compare_and_fusion.3 = (pred[3]{0:T(512)(128)(4,1)S(1)}, pred[3]{0:T(512)(128)(4,1)}) fusion(pred[3]{0:T(512)(128)(4,1)S(1)} %get-tuple-element.6, s32[]{:T(128)} %bitcast.38, pred[3]{0:T(512)(128)(4,1)S(1)} %get-tuple-element.7, s32[]{:T(128)} %bitcast.22), kind=kLoop, calls=%fused_computation.119 | loop fusion | flops 12 | bytes 20 | tf_op jit(solution)/shard_map/and | solution.py:55
  14.0 3.9 %gather_fusion.2 = bf16[4,2,384,384]{3,2,1,0:T(8,128)(2,1)} fusion(bf16[3,2,384,384]{3,2,1,0:T(8,128)(2,1)} %bitcast.174, s32[1024]{0:T(1024)S(1)} %pad_clamp_fusion), kind=kCustom, calls=%fused_computation.2.clone | custom fusion | bytes 4718608 | tf_op jit(solution)/shard_map/jit(_take)/gather | solution.py:58
  17.9 1.5 %bitcast_select_fusion = bf16[1,3,2,384,384]{4,3,1,2,0:T(8,128)(2,1)S(1)} fusion(bf16[1,1,3,2,384,384]{5,4,3,2,1,0:T(8,128)(2,1)S(1)} %copy-done.6, pred[3,384,384]{2,1,0:T(8,128)(4,1)} %broadcast_and_fusion), kind=kLoop, calls=%fused_computation.10 | loop fusion | flops 884736 | bytes 3981312 | tf_op jit(solution)/shard_map/jit(_where)/select_n | solution.py:75
  19.7 1.8 %fusion = bf16[4,2,384,384]{3,2,0,1:T(8,128)(2,1)} fusion(bf16[4,2,384,384]{3,2,1,0:T(8,128)(2,1)S(1)} %copy-done.2, pred[4]{0:T(512)(128)(4,1)S(1)} %copy-done.7, bf16[4]{0:T(256)(128)(2,1)S(1)} %copy-done.8), kind=kLoop, calls=%fused_computation.5 | loop fusion | flops 2359296 | bytes 4718604 | tf_op jit(solution)/shard_map/mul | solution.py:58
  22.1 2.3 %gather_fusion.1 = bf16[4,2,384,384]{3,2,1,0:T(8,128)(2,1)} fusion(bf16[3,2,384,384]{3,2,1,0:T(8,128)(2,1)S(1)} %bitcast.175, s32[1024]{0:T(1024)S(1)} %pad_clamp_fusion.1), kind=kCustom, calls=%fused_computation.1.clone | custom fusion | bytes 4718608 | tf_op jit(solution)/shard_map/jit(_take)/gather | solution.py:58
  24.5 1.3 %compare_and_fusion.5 = pred[3]{0:T(512)(128)(4,1)S(1)} fusion(pred[3]{0:T(512)(128)(4,1)} %get-tuple-element.8, s32[]{:T(128)} %bitcast.6), kind=kLoop, calls=%fused_computation.121 | loop fusion | flops 6 | bytes 10 | tf_op jit(solution)/shard_map/and | solution.py:55
  25.8 3.5 %fusion.1 = bf16[4,2,384,384]{3,2,0,1:T(8,128)(2,1)} fusion(bf16[4,2,384,384]{3,2,1,0:T(8,128)(2,1)} %gather_fusion.1, pred[4]{0:T(512)(128)(4,1)} %get-tuple-element.23, bf16[4]{0:T(256)(128)(2,1)} %fusion.53), kind=kLoop, calls=%fused_computation.7 | loop fusion | flops 2359296 | bytes 4718604 | tf_op jit(solution)/shard_map/mul | solution.py:58
  29.2 1.4 %multiply_convert_fusion = bf16[1,1,2,384,384]{4,3,1,2,0:T(8,128)(2,1)S(1)} fusion(bf16[1,1,2,384,384]{4,3,1,2,0:T(8,128)(2,1)} %collective-permute-done.1, bf16[1,1,2,384,384]{4,3,1,2,0:T(8,128)(2,1)} %collective-permute-done), kind=kLoop, calls=%fused_computation.61 | loop fusion | flops 1474560 | bytes 1769472 | tf_op jit(solution)/shard_map/convert_element_type | solution.py:68
  30.7 2.6 %fusion.55 = (bf16[4,2,384,384]{3,2,0,1:T(8,128)(2,1)}, bf16[1,4,2,384,384]{4,3,1,2,0:T(8,128)(2,1)}) fusion(bf16[1,1,2,384,384]{4,3,1,2,0:T(8,128)(2,1)S(1)} %multiply_convert_fusion, bf16[1,3,2,384,384]{4,3,1,2,0:T(8,128)(2,1)S(1)} %bitcast_select_fusion), kind=kLoop, calls=%fused_computation.122 | loop fusion | flops 1179648 | bytes 7077888 | tf_op jit(solution)/shard_map/squeeze | solution.py:84
  33.3 4.5 %collective-permute-start.3 = (bf16[1,4,2,384,384]{4,3,1,2,0:T(8,128)(2,1)}, bf16[1,4,2,384,384]{4,3,1,2,0:T(8,128)(2,1)}, u32[]{:S(2)}, u32[]{:S(2)}) collective-permute-start(bf16[1,4,2,384,384]{4,3,1,2,0:T(8,128)(2,1)} %get-tuple-element.19), channel_id=1, source_target_pairs={{8,0},{16,8},{24,16},{32,24},{40,32},{48,40},{56,48},{64,56},{72,6... | collective-permute-start | bytes 7077896 | tf_op jit(solution)/shard_map/ppermute | solution.py:21
  37.8 2.4 %gather_fusion = bf16[4,2,384,384]{3,2,1,0:T(8,128)(2,1)} fusion(bf16[3,2,384,384]{3,2,1,0:T(8,128)(2,1)S(1)} %bitcast.176, s32[1024]{0:T(1024)S(1)} %pad_clamp_fusion.2), kind=kCustom, calls=%fused_computation.clone | custom fusion | bytes 4718608 | tf_op jit(solution)/shard_map/jit(_take)/gather | solution.py:58
  40.2 2.2 %fusion.2 = bf16[4,2,384,384]{3,2,0,1:T(8,128)(2,1)S(1)} fusion(bf16[4,2,384,384]{3,2,1,0:T(8,128)(2,1)} %gather_fusion, pred[4]{0:T(512)(128)(4,1)S(1)} %get-tuple-element.16, bf16[4]{0:T(256)(128)(2,1)S(1)} %fusion.52), kind=kLoop, calls=%fused_computation.9 | loop fusion | flops 2359296 | bytes 4718604 | tf_op jit(solution)/shard_map/mul | solution.py:58
  42.4 2.1 %collective-permute-start.2 = (bf16[1,4,2,384,384]{4,3,1,2,0:T(8,128)(2,1)}, bf16[1,4,2,384,384]{4,3,1,2,0:T(8,128)(2,1)S(1)}, u32[]{:S(2)}, u32[]{:S(2)}) collective-permute-start(bf16[1,4,2,384,384]{4,3,1,2,0:T(8,128)(2,1)} %get-tuple-element.19), channel_id=1, source_target_pairs={{0,8},{8,16},{16,24},{24,32},{32,40},{40,48},{48,56},{56,64},{64,7... | collective-permute-start | bytes 7077896 | tf_op jit(solution)/shard_map/ppermute | solution.py:18
  44.6 0.8 convolution_bitcast_fusion.6
  45.4 0.8 fusion.18
  46.6 0.8 convolution_bitcast_fusion.4
  47.4 0.8 fusion.17
  49.4 39.2 %collective-permute-done.3 = bf16[1,4,2,384,384]{4,3,1,2,0:T(8,128)(2,1)} collective-permute-done((bf16[1,4,2,384,384]{4,3,1,2,0:T(8,128)(2,1)}, bf16[1,4,2,384,384]{4,3,1,2,0:T(8,128)(2,1)}, u32[]{:S(2)}, u32[]{:S(2)}) %collective-permute-start.3) | collective-permute-done | bytes 2359328 | tf_op jit(solution)/shard_map/ppermute | solution.py:21
  88.6 2.1 %convolution_bitcast_fusion.2 = f32[384,384]{1,0:T(8,128)S(1)} fusion(bf16[4,2,384,384]{3,2,0,1:T(8,128)(2,1)} %bitcast.36, bf16[4,2,384,384]{3,2,0,1:T(8,128)(2,1)S(1)} %copy-done.4), kind=kOutput, calls=%fused_computation.17 | convolution fusion | flops 452984832 | bytes 2949120 | tf_op jit(solution)/shard_map/dot_general | solution.py:30
  90.6 2.1 %convolution_bitcast_fusion = f32[384,384]{1,0:T(8,128)S(1)} fusion(bf16[4,2,384,384]{3,2,0,1:T(8,128)(2,1)} %bitcast.36, bf16[4,2,384,384]{3,2,0,1:T(8,128)(2,1)S(1)} %copy-done.4), kind=kOutput, calls=%fused_computation.15 | convolution fusion | flops 452984832 | bytes 2949120 | tf_op jit(solution)/shard_map/dot_general | solution.py:30
  92.7 7.9 %collective-permute-done.2 = bf16[1,4,2,384,384]{4,3,1,2,0:T(8,128)(2,1)S(1)} collective-permute-done((bf16[1,4,2,384,384]{4,3,1,2,0:T(8,128)(2,1)}, bf16[1,4,2,384,384]{4,3,1,2,0:T(8,128)(2,1)S(1)}, u32[]{:S(2)}, u32[]{:S(2)}) %collective-permute-start.2) | collective-permute-done | bytes 2359328 | tf_op jit(solution)/shard_map/ppermute | solution.py:18
  102.2 2.1 %fusion.16 = bf16[384,384]{1,0:T(8,128)(2,1)S(1)} fusion(f32[384,384]{1,0:T(8,128)S(1)} %convolution_bitcast_fusion.2, bf16[4,2,384,384]{3,2,0,1:T(8,128)(2,1)} %bitcast.36, bf16[4,2,384,384]{3,2,0,1:T(8,128)(2,1)S(1)} %copy-done.4), kind=kOutput, calls=%fused_computation.42 | convolution fusion | flops 453279744 | bytes 3244032 | tf_op jit(solution)/shard_map/dot_general | solution.py:30
  104.7 2.1 %fusion.15 = bf16[384,384]{1,0:T(8,128)(2,1)S(1)} fusion(f32[384,384]{1,0:T(8,128)S(1)} %convolution_bitcast_fusion, bf16[4,2,384,384]{3,2,0,1:T(8,128)(2,1)S(1)} %copy-done.4, bf16[4,2,384,384]{3,2,0,1:T(8,128)(2,1)} %bitcast.36), kind=kOutput, calls=%fused_computation.41 | convolution fusion | flops 453279744 | bytes 3244032 | tf_op jit(solution)/shard_map/dot_general | solution.py:30
  108.0 0.8 fusion.20
  109.2 0.8 fusion.19
  111.4 1.4 %copy.17 = f32[1,1,2,384,384]{4,3,2,1,0:T(8,128)} copy(f32[1,1,2,384,384]{3,4,2,1,0:T(8,128)S(1)} %fusion.21) | data formatting | bytes 2359296 | tf_op jit(solution)/shard_map/add | solution.py:82
  (47 shorter events, 9.2 us)
Async XLA Ops:
  0.0 10.4 %copy-start = (s32[32,3]{0,1:T(4,128)S(1)}, s32[32,3]{0,1:T(4,128)}, u32[]{:S(2)}) copy-start(s32[32,3]{0,1:T(4,128)} %param.13) | copy-start | bytes 1156
  0.0 29.2 %collective-permute-start = (bf16[1,1,2,384,384]{4,3,1,2,0:T(8,128)(2,1)}, bf16[1,1,2,384,384]{4,3,1,2,0:T(8,128)(2,1)}, u32[]{:S(2)}, u32[]{:S(2)}) collective-permute-start(bf16[1,1,2,384,384]{4,3,1,2,0:T(8,128)(2,1)} %bitcast.181), channel_id=1, source_target_pairs={{0,1},{1,2},{2,3},{3,4},{4,5},{5,6},{6,7},{8,9},{9,10},{10,11},{11... | collective-permute-start | bytes 1769480 | tf_op jit(solution)/shard_map/ppermute | solution.py:10
  2.1 27.2 %collective-permute-start.1 = (bf16[1,1,2,384,384]{4,3,1,2,0:T(8,128)(2,1)}, bf16[1,1,2,384,384]{4,3,1,2,0:T(8,128)(2,1)}, u32[]{:S(2)}, u32[]{:S(2)}) collective-permute-start(bf16[1,1,2,384,384]{4,3,1,2,0:T(8,128)(2,1)} %bitcast.182), channel_id=1, source_target_pairs={{1,0},{2,1},{3,2},{4,3},{5,4},{6,5},{7,6},{9,8},{10,9},{11,10},{12... | collective-permute-start | bytes 1769480 | tf_op jit(solution)/shard_map/ppermute | solution.py:10
  14.0 3.9 %copy-start.6 = (bf16[1,1,3,2,384,384]{5,4,3,2,1,0:T(8,128)(2,1)S(1)}, bf16[1,1,3,2,384,384]{5,4,3,2,1,0:T(8,128)(2,1)}, u32[]{:S(2)}) copy-start(bf16[1,1,3,2,384,384]{5,4,3,2,1,0:T(8,128)(2,1)} %param.9) | copy-start | bytes 5308420
  17.9 1.8 %copy-start.2 = (bf16[4,2,384,384]{3,2,1,0:T(8,128)(2,1)S(1)}, bf16[4,2,384,384]{3,2,1,0:T(8,128)(2,1)}, u32[]{:S(2)}) copy-start(bf16[4,2,384,384]{3,2,1,0:T(8,128)(2,1)} %gather_fusion.2) | copy-start | bytes 7077892
  17.9 1.8 %copy-start.7 = (pred[4]{0:T(512)(128)(4,1)S(1)}, pred[4]{0:T(512)(128)(4,1)}, u32[]{:S(2)}) copy-start(pred[4]{0:T(512)(128)(4,1)} %get-tuple-element.12) | copy-start | bytes 16
  17.9 1.8 %copy-start.8 = (bf16[4]{0:T(256)(128)(2,1)S(1)}, bf16[4]{0:T(256)(128)(2,1)}, u32[]{:S(2)}) copy-start(bf16[4]{0:T(256)(128)(2,1)} %fusion.54) | copy-start | bytes 28
  19.7 1.8 %copy-start.9 = (pred[3]{0:T(512)(128)(4,1)S(1)}, pred[3]{0:T(512)(128)(4,1)}, u32[]{:S(2)}) copy-start(pred[3]{0:T(512)(128)(4,1)} %get-tuple-element.26) | copy-start | bytes 13
  19.7 2.4 %copy-start.1 = (bf16[1,1,3,2,384,384]{5,4,3,2,1,0:T(8,128)(2,1)S(1)}, bf16[1,1,3,2,384,384]{5,4,3,2,1,0:T(8,128)(2,1)}, u32[]{:S(2)}) copy-start(bf16[1,1,3,2,384,384]{5,4,3,2,1,0:T(8,128)(2,1)} %param.8) | copy-start | bytes 5308420
  33.3 55.3 %collective-permute-start.3 = (bf16[1,4,2,384,384]{4,3,1,2,0:T(8,128)(2,1)}, bf16[1,4,2,384,384]{4,3,1,2,0:T(8,128)(2,1)}, u32[]{:S(2)}, u32[]{:S(2)}) collective-permute-start(bf16[1,4,2,384,384]{4,3,1,2,0:T(8,128)(2,1)} %get-tuple-element.19), channel_id=1, source_target_pairs={{8,0},{16,8},{24,16},{32,24},{40,32},{48,40},{56,48},{64,56},{72,6... | collective-permute-start | bytes 7077896 | tf_op jit(solution)/shard_map/ppermute | solution.py:21
  40.2 4.3 %copy-start.3 = (bf16[4,2,384,384]{3,2,0,1:T(8,128)(2,1)S(1)}, bf16[4,2,384,384]{3,2,0,1:T(8,128)(2,1)}, u32[]{:S(2)}) copy-start(bf16[4,2,384,384]{3,2,0,1:T(8,128)(2,1)} %get-tuple-element.18) | copy-start | bytes 7077892
  40.2 4.3 %copy-start.5 = (bf16[4,2,384,384]{3,2,0,1:T(8,128)(2,1)S(1)}, bf16[4,2,384,384]{3,2,0,1:T(8,128)(2,1)}, u32[]{:S(2)}) copy-start(bf16[4,2,384,384]{3,2,0,1:T(8,128)(2,1)} %fusion.1) | copy-start | bytes 7077892
  42.4 58.2 %collective-permute-start.2 = (bf16[1,4,2,384,384]{4,3,1,2,0:T(8,128)(2,1)}, bf16[1,4,2,384,384]{4,3,1,2,0:T(8,128)(2,1)S(1)}, u32[]{:S(2)}, u32[]{:S(2)}) collective-permute-start(bf16[1,4,2,384,384]{4,3,1,2,0:T(8,128)(2,1)} %get-tuple-element.19), channel_id=1, source_target_pairs={{0,8},{8,16},{16,24},{24,32},{32,40},{40,48},{48,56},{56,64},{64,7... | collective-permute-start | bytes 7077896 | tf_op jit(solution)/shard_map/ppermute | solution.py:18
  48.6 40.0 %copy-start.4 = (bf16[4,2,384,384]{3,2,0,1:T(8,128)(2,1)S(1)}, bf16[4,2,384,384]{3,2,0,1:T(8,128)(2,1)}, u32[]{:S(2)}) copy-start(bf16[4,2,384,384]{3,2,0,1:T(8,128)(2,1)} %fusion) | copy-start | bytes 7077892
where the time goes:
time: 113 us
  waiting for transfers between devices  47.1 us (42%)
  other arithmetic  21.8 us (19%)
  matrix products  19.4 us (17%)
  starting transfers between devices  12.2 us (11%)
  local copies, waits for them, and re-layouts  11.9 us (11%)
    ppermute x1, waiting for transfers between devices, extended_2(): lax.ppermute(lax.slice_in_dim(block, 0, width, axis=dim), axis, backward)  39.2 us
    dot_general x12, matrix products, pair_dot(): lax.dot_general(left, right, layout, preferred_element_type=jnp.float32)  14.6 us
    gather x3, local copies, waits for them, and re-layouts, slab_term(): chosen = jnp.take(green_row, pick, axis=0) * keep[:, None, None, None]  8.61 us
    ppermute x1, waiting for transfers between devices, extended_2(): lax.ppermute(lax.slice_in_dim(block, block.shape[dim] - width, None, axis...  7.89 us
    mul x3, other arithmetic, slab_term(): chosen = jnp.take(green_row, pick, axis=0) * keep[:, None, None, None]  7.47 us
    ppermute x2, starting transfers between devices, from_behind(): lax.ppermute(value, axis, [(source, source + steps) for source in range(l...  5.68 us
    and x3, other arithmetic, slab_term(): usable = (place >= 0) & (place <= 2) & (slot_ids < count)  4.52 us
    ppermute x1, starting transfers between devices, extended_2(): lax.ppermute(lax.slice_in_dim(block, 0, width, axis=dim), axis, backward)  4.46 us
  transfers between devices with their start and end apart: 4, of which 2 were waited for; matrix products, arithmetic and copies ran while one was open for 33% of the time, Pallas kernels for 0%

commit v1 on v0

v1 whole, which is shorter than its diff:
```python
import jax
import jax.numpy as jnp
from jax import lax
from jax.experimental import pallas as pl
from jax.experimental.pallas import tpu as pltpu
from jax.sharding import PartitionSpec as P

F32 = jnp.float32
BF16 = jnp.bfloat16
VMEM_LIMIT = 24 * 1024 * 1024


def cost(flops, moved):
    return pl.CostEstimate(flops=int(flops), bytes_accessed=int(moved), transcendentals=0)


def dot(left, right):
    return jnp.dot(left, right, preferred_element_type=F32)


def pair_limit(slab, offset, q, off, cnt, rng):
    live = (off[slab, q] == offset) & (q < cnt[slab])
    return jnp.where(live, rng[slab, q], 0)


def merged(slab, offset, sigma, part, rows, cols, off, cnt, rng):
    total = jnp.zeros(rows.shape, F32)
    for q in range(sigma.shape[2]):
        limit = pair_limit(slab, offset, q, off, cnt, rng)
        inside = (rows < limit) & (cols < limit)
        total = total + jnp.where(inside, sigma[0, 0, q, part].astype(F32), 0.0)
    return total


def index_grid(first, height, width):
    rows = lax.broadcasted_iota(jnp.int32, (height, width), 0) + first
    cols = lax.broadcasted_iota(jnp.int32, (height, width), 1)
    return rows, cols


def side_kernel(off, cnt, rng, sigma, low, high):
    slab = lax.axis_index("slab")
    height, width = sigma.shape[-2:]
    rows, cols = index_grid(pl.program_id(0) * height, height, width)
    for out, offsets in ((low, (-2, -1)), (high, (1, 2))):
        for slot, offset in enumerate(offsets):
            for part in range(2):
                block = merged(slab, offset, sigma, part, rows, cols, off, cnt, rng)
                at = (2 * slot + part) * width
                out[:, at : at + width] = block.astype(BF16)


def centre_kernel(off, cnt, rng, sigma, below, above, out):
    slab = lax.axis_index("slab")
    height, width = sigma.shape[-2:]
    rows, cols = index_grid(pl.program_id(0) * height, height, width)
    for part in range(2):
        block = merged(slab, 0, sigma, part, rows, cols, off, cnt, rng)
        mixed = 0.5 * (below[0, 0, part].astype(F32) + above[0, 0, part].astype(F32))
        block = block + mixed.astype(BF16).astype(F32)
        out[:, part * width : (part + 1) * width] = block.astype(BF16)


def green_kernel(green, right, left):
    width = green.shape[-1]
    for o in range(3):
        real, imag = green[0, 0, o, 0], green[0, 0, o, 1]
        real_t, imag_t = real.T, imag.T
        at = 2 * o * width
        right[at : at + width, :width] = real_t
        right[at : at + width, width:] = -imag_t
        right[at + width : at + 2 * width, :width] = imag_t
        right[at + width : at + 2 * width, width:] = real_t
        to = 2 * ((o + 1) % 3) * width
        left[:, to : to + width] = real
        left[:, to + width : to + 2 * width] = imag


def spread(x, out, first):
    width = x.shape[1] // 2
    rounded = x.astype(BF16)
    real, imag = rounded[:, :width], rounded[:, width:]
    out[first : first + width, :width] = real
    out[first : first + width, width:] = imag
    out[first + width : first + 2 * width, :width] = -imag
    out[first + width : first + 2 * width, width:] = real


def local_kernel(low, centre, high, right, left, out, held):
    wide = centre.shape[1]
    x = dot(low[:, wide:], right[:wide])
    x = x + dot(centre[...], right[wide : 2 * wide])
    x = x + dot(high[:, :wide], right[2 * wide :])
    spread(x, held, 0)
    out[...] = dot(left[:, 2 * wide :], held[...])


def arrive_kernel(from_above, from_below, right, out_above, out_below):
    wide = from_above.shape[1]
    out_above[...] = dot(from_above[...], right[:wide])
    out_below[...] = dot(from_below[...], right[wide // 2 :])


def finish_kernel(centre_above, centre_below, x_above, x_below, right, left, partial, out, held):
    wide = centre_above.shape[1]
    width = wide // 2
    above = x_above[...] + dot(centre_above[...], right[2 * wide :])
    below = x_below[...] + dot(centre_below[...], right[:wide])
    spread(above, held, 0)
    spread(below, held, wide)
    total = partial[...] + dot(left[:, : 2 * wide], held[...])
    out[0, 0, 0] = total[:, :width]
    out[0, 0, 1] = total[:, width:]


def smem():
    return pl.BlockSpec(memory_space=pltpu.SMEM)


def params():
    return pltpu.CompilerParams(vmem_limit_bytes=VMEM_LIMIT)


def body(green, sigma, phonon, pair_off, pair_count, pair_range):
    width = green.shape[-1]
    wide = 2 * width
    slots = sigma.shape[2]
    slabs = lax.axis_size("slab")
    points = lax.axis_size("energy")
    up = [(i, i + 1) for i in range(slabs - 1)]
    down = [(i + 1, i) for i in range(slabs - 1)]
    energy_up = [(i, i + 1) for i in range(points - 1)]
    energy_down = [(i + 1, i) for i in range(points - 1)]
    tables = (pair_off, pair_count, pair_range)

    ph_below = lax.ppermute(phonon, "energy", energy_up)
    ph_above = lax.ppermute(phonon, "energy", energy_down)

    height = 128
    steps = width // height
    sigma_spec = pl.BlockSpec((1, 1, slots, 2, height, width), lambda s: (0, 0, 0, 0, s, 0))
    phonon_spec = pl.BlockSpec((1, 1, 2, height, width), lambda s: (0, 0, 0, s, 0))
    side_spec = pl.BlockSpec((height, 2 * wide), lambda s: (s, 0))
    block_bytes = 2 * width * wide
    low, high = pl.pallas_call(
        side_kernel,
        grid=(steps,),
        in_specs=[smem(), smem(), smem(), sigma_spec],
        out_specs=[side_spec, side_spec],
        out_shape=[jax.ShapeDtypeStruct((width, 2 * wide), BF16)] * 2,
        compiler_params=params(),
        cost_estimate=cost(3e9, 7 * block_bytes),
        name="side",
    )(*tables, sigma)
    low_above = lax.ppermute(low, "slab", down)
    high_below = lax.ppermute(high, "slab", up)

    centre = pl.pallas_call(
        centre_kernel,
        grid=(steps,),
        in_specs=[smem(), smem(), smem(), sigma_spec, phonon_spec, phonon_spec],
        out_specs=pl.BlockSpec((height, wide), lambda s: (s, 0)),
        out_shape=jax.ShapeDtypeStruct((width, wide), BF16),
        compiler_params=params(),
        cost_estimate=cost(3e9, 6 * block_bytes),
        name="centre",
    )(*tables, sigma, ph_below, ph_above)
    centre_above = lax.ppermute(centre, "slab", down)
    centre_below = lax.ppermute(centre, "slab", up)

    right, left = pl.pallas_call(
        green_kernel,
        out_shape=[
            jax.ShapeDtypeStruct((3 * wide, wide), BF16),
            jax.ShapeDtypeStruct((width, 3 * wide), BF16),
        ],
        compiler_params=params(),
        cost_estimate=cost(4e9, 12 * block_bytes),
        name="green",
    )(green)

    square = jax.ShapeDtypeStruct((width, wide), F32)
    partial = pl.pallas_call(
        local_kernel,
        out_shape=square,
        scratch_shapes=[pltpu.VMEM((wide, wide), BF16)],
        compiler_params=params(),
        cost_estimate=cost(2 * width * wide * 4 * wide, 16 * block_bytes),
        name="local",
    )(low, centre, high, right, left)

    x_above, x_below = pl.pallas_call(
        arrive_kernel,
        out_shape=[square, square],
        compiler_params=params(),
        cost_estimate=cost(2 * width * wide * 4 * wide, 16 * block_bytes),
        name="arrive",
    )(low_above, high_below, right)

    return pl.pallas_call(
        finish_kernel,
        out_shape=jax.ShapeDtypeStruct((1, 1, 2, width, width), F32),
        scratch_shapes=[pltpu.VMEM((2 * wide, wide), BF16)],
        compiler_params=params(),
        cost_estimate=cost(2 * width * wide * 4 * wide, 16 * block_bytes),
        name="finish",
    )(centre_above, centre_below, x_above, x_below, right, left, partial)


def solution(mesh):
    in_specs = (
        P("energy", "slab", None, None, None, None),
        P("energy", "slab", None, None, None, None),
        P("energy", "slab", None, None, None),
        P(),
        P(),
        P(),
    )
    out_specs = P("energy", "slab", None, None, None)
    return jax.shard_map(body, mesh=mesh, in_specs=in_specs, out_specs=out_specs, check_vma=False)
```

time: 113 us -> 66.1 us (0.58)
  other arithmetic: 21.8 us -> 0 us
  waiting for transfers between devices: 47.1 us -> 26.5 us
  matrix products: 19.4 us -> 0 us
  Pallas kernels: 0 us -> 14.2 us
  starting transfers between devices: 12.2 us -> 21.2 us
  local copies, waits for them, and re-layouts: 11.9 us -> 3.66 us
    ppermute x4 -> x6, waiting for transfers between devices: 47.1 us -> 26.5 us  [the longest x1 9.38 us: body(): low_above = lax.ppermute(low, 'slab', down)]
    dot_general x24 -> x0, matrix products: 19.4 us -> none  [the longest x12 14.6 us: pair_dot(): lax.dot_general(left, right, layout, preferred_element_type=jnp.float32)]
    pallas_call x0 -> x6, Pallas kernels: none -> 14.2 us  [the longest x1 3.32 us: body(): pl.pallas_call(side_kernel, grid=(steps,), in_specs=[smem(), smem(), smem...]
    ppermute x4 -> x6, starting transfers between devices: 12.2 us -> 21.2 us  [the longest x1 7.24 us: body(): centre_above = lax.ppermute(centre, 'slab', down)]
    gather x3 -> x0, local copies, waits for them, and re-layouts: 8.61 us -> none  [slab_term(): chosen = jnp.take(green_row, pick, axis=0) * keep[:, None, None, None]]
    mul x3 -> x0, other arithmetic: 7.47 us -> none  [slab_term(): chosen = jnp.take(green_row, pick, axis=0) * keep[:, None, None, None]]
    and x6 -> x0, other arithmetic: 6.3 us -> none  [the longest x3 4.52 us: slab_term(): usable = (place >= 0) & (place <= 2) & (slot_ids < count)]
    unnamed x20 -> x8, local copies, waits for them, and re-layouts: 0.3 us -> 3.66 us
  transfers between devices with their start and end apart: 4 -> 6, of which waited for: 2 -> 4; matrix products, arithmetic and copies ran while one was open for 33% -> 2% of each run, Pallas kernels for 0% -> 17%
where the time goes in v1:
time: 66.1 us; the launch traced here: 65.8 us
  waiting for transfers between devices  26.5 us (40%)
  starting transfers between devices  21.2 us (32%)
  Pallas kernels  14.2 us (21%)
  local copies, waits for them, and re-layouts  3.66 us (6%)
    ppermute x1, waiting for transfers between devices, body(): low_above = lax.ppermute(low, 'slab', down)  9.38 us
    ppermute x1, waiting for transfers between devices, body(): high_below = lax.ppermute(high, 'slab', up)  7.86 us
    ppermute x1, waiting for transfers between devices, body(): centre_below = lax.ppermute(centre, 'slab', up)  7.58 us
    ppermute x1, starting transfers between devices, body(): centre_above = lax.ppermute(centre, 'slab', down)  7.24 us
    ppermute x1, starting transfers between devices, body(): low_above = lax.ppermute(low, 'slab', down)  4.47 us
    unnamed x8, local copies, waits for them, and re-layouts  3.66 us
    ppermute x1, starting transfers between devices, body(): ph_above = lax.ppermute(phonon, 'energy', energy_down)  3.64 us
    pallas_call x1, Pallas kernels, body(): pl.pallas_call(side_kernel, grid=(steps,), in_specs=[smem(), smem(), smem...  3.32 us
  transfers between devices with their start and end apart: 6, of which 4 were waited for; matrix products, arithmetic and copies ran while one was open for 2% of the time, Pallas kernels for 17%

profile of v1, /device:TPU:130, one launch (start us, length us, event | category | flops | bytes accessed | tf_op | source)
XLA Modules:
  0.0 65.8 jit_solution(16155954075805413357)
XLA Ops:
  0.0 1.9 %collective-permute-start = (bf16[1,1,2,384,384]{4,3,2,1,0:T(8,128)(2,1)}, bf16[1,1,2,384,384]{4,3,2,1,0:T(8,128)(2,1)S(1)}, u32[]{:S(2)}, u32[]{:S(2)}) collective-permute-start(bf16[1,1,2,384,384]{4,3,2,1,0:T(8,128)(2,1)} %param.8), channel_id=1, source_target_pairs={{0,1},{1,2},{2,3},{3,4},{4,5},{5,6},{6,7},{8,9},{9,10},{10,11},{11... | collective-permute-start | bytes 1769480 | tf_op jit(solution)/shard_map/ppermute | solution.py:136
  1.9 3.6 %collective-permute-start.1 = (bf16[1,1,2,384,384]{4,3,2,1,0:T(8,128)(2,1)}, bf16[1,1,2,384,384]{4,3,2,1,0:T(8,128)(2,1)S(1)}, u32[]{:S(2)}, u32[]{:S(2)}) collective-permute-start(bf16[1,1,2,384,384]{4,3,2,1,0:T(8,128)(2,1)} %param.8), channel_id=1, source_target_pairs={{1,0},{2,1},{3,2},{4,3},{5,4},{6,5},{7,6},{9,8},{10,9},{11,10},{12... | collective-permute-start | bytes 1769480 | tf_op jit(solution)/shard_map/ppermute | solution.py:137
  5.6 0.8 %copy.7.off = s32[32,3]{1,0:T(8,128)S(1)} copy(s32[32,3]{0,1:T(4,128)} %param.9) | data formatting | bytes 768 | tf_op args[3]
  6.3 0.8 %copy.8.rng = s32[32,3]{1,0:T(8,128)S(1)} copy(s32[32,3]{0,1:T(4,128)} %param.11) | data formatting | bytes 768 | tf_op args[5]
  7.1 0.0 copy-start
  7.1 1.5 %copy-done = bf16[1,1,3,2,384,384]{5,4,3,2,1,0:T(8,128)(2,1)S(1)} copy-done((bf16[1,1,3,2,384,384]{5,4,3,2,1,0:T(8,128)(2,1)S(1)}, bf16[1,1,3,2,384,384]{5,4,3,2,1,0:T(8,128)(2,1)}, u32[]{:S(2)}) %copy-start) | copy-done | bytes 1769496
  8.6 0.0 copy-start.2
  8.6 0.7 copy-done.2
  9.2 3.3 %side.1 = (bf16[384,1536]{1,0:T(8,128)(2,1)S(1)}, bf16[384,1536]{1,0:T(8,128)(2,1)S(1)}) custom-call(s32[32,3]{1,0:T(8,128)S(1)} %copy.7.off, s32[32]{0:T(128)S(1)} %copy-done.2, s32[32,3]{1,0:T(8,128)S(1)} %copy.8.rng, bf16[1,1,3,2,384,384]{5,4,3,2,1,0:T(8,128)(2,1)S(1)} %copy-done), custom_call_target="tpu_custom_call" | custom-call | flops 3000000000 | bytes 4128768 | tf_op jit(solution)/shard_map/side/pallas_call | solution.py:145
  12.6 4.5 %collective-permute-start.4 = (bf16[384,1536]{1,0:T(8,128)(2,1)S(1)}, bf16[384,1536]{1,0:T(8,128)(2,1)S(1)}, u32[]{:S(2)}, u32[]{:S(2)}) collective-permute-start(bf16[384,1536]{1,0:T(8,128)(2,1)S(1)} %get-tuple-element.11.low), channel_id=1, source_target_pairs={{8,0},{16,8},{24,16},{32,24},{40,32},{48,40},{56,48},{64,56},{72,6... | collective-permute-start | bytes 3538952 | tf_op jit(solution)/shard_map/ppermute | solution.py:155
  17.0 0.0 copy-start.1
  17.0 2.1 %collective-permute-start.5 = (bf16[384,1536]{1,0:T(8,128)(2,1)S(1)}, bf16[384,1536]{1,0:T(8,128)(2,1)S(1)}, u32[]{:S(2)}, u32[]{:S(2)}) collective-permute-start(bf16[384,1536]{1,0:T(8,128)(2,1)S(1)} %get-tuple-element.12.high), channel_id=1, source_target_pairs={{0,8},{8,16},{16,24},{24,32},{32,40},{40,48},{48,56},{56,64},{64,7... | collective-permute-start | bytes 3538952 | tf_op jit(solution)/shard_map/ppermute | solution.py:156
  19.1 0.0 collective-permute-done.below
  19.1 0.0 collective-permute-done.1.above
  19.1 2.2 %centre.1 = bf16[384,768]{1,0:T(8,128)(2,1)S(1)} custom-call(s32[32,3]{1,0:T(8,128)S(1)} %copy.7.off, s32[32]{0:T(128)S(1)} %copy-done.2, s32[32,3]{1,0:T(8,128)S(1)} %copy.8.rng, bf16[1,1,3,2,384,384]{5,4,3,2,1,0:T(8,128)(2,1)S(1)} %copy-done, bf16[1,1,2,384,384]{4,3,2,1,0:T(8,128)(2,1)S(1)} %collective-permute-done.below, ...), custom_call_target="tpu_custom_call" | custom-call | flops 3000000000 | bytes 3538944 | tf_op jit(solution)/shard_map/centre/pallas_call | solution.py:158
  21.3 7.2 %collective-permute-start.2 = (bf16[384,768]{1,0:T(8,128)(2,1)S(1)}, bf16[384,768]{1,0:T(8,128)(2,1)S(1)}, u32[]{:S(2)}, u32[]{:S(2)}) collective-permute-start(bf16[384,768]{1,0:T(8,128)(2,1)S(1)} %centre.1), channel_id=1, source_target_pairs={{8,0},{16,8},{24,16},{32,24},{40,32},{48,40},{56,48},{64,56},{72,6... | collective-permute-start | bytes 1769480 | tf_op jit(solution)/shard_map/ppermute | solution.py:168
  28.6 1.9 %collective-permute-start.3 = (bf16[384,768]{1,0:T(8,128)(2,1)S(1)}, bf16[384,768]{1,0:T(8,128)(2,1)S(1)}, u32[]{:S(2)}, u32[]{:S(2)}) collective-permute-start(bf16[384,768]{1,0:T(8,128)(2,1)S(1)} %centre.1), channel_id=1, source_target_pairs={{0,8},{8,16},{16,24},{24,32},{32,40},{40,48},{48,56},{56,64},{64,7... | collective-permute-start | bytes 1769480 | tf_op jit(solution)/shard_map/ppermute | solution.py:169
  30.5 0.0 copy-done.1
  30.5 0.6 green.2
  31.1 2.9 %local.1.partial = f32[384,768]{1,0:T(8,128)S(1)} custom-call(bf16[384,1536]{1,0:T(8,128)(2,1)S(1)} %get-tuple-element.11.low, bf16[384,768]{1,0:T(8,128)(2,1)S(1)} %centre.1, bf16[384,1536]{1,0:T(8,128)(2,1)S(1)} %get-tuple-element.12.high, bf16[2304,768]{1,0:T(8,128)(2,1)S(1)} %get-tuple-element.13.right, bf16[384,2304]{1,0:T(8,128)(2,1)S(1)} %get-tuple-element.16.left), custom_call_target="tpu_custom_call" | custom-call | flops 1811939328 | bytes 9437184 | tf_op jit(solution)/shard_map/local/pallas_call | solution.py:183
  34.0 9.4 %collective-permute-done.4.from_above = bf16[384,1536]{1,0:T(8,128)(2,1)S(1)} collective-permute-done((bf16[384,1536]{1,0:T(8,128)(2,1)S(1)}, bf16[384,1536]{1,0:T(8,128)(2,1)S(1)}, u32[]{:S(2)}, u32[]{:S(2)}) %collective-permute-start.4) | collective-permute-done | bytes 1179680 | tf_op jit(solution)/shard_map/ppermute | solution.py:155
  43.4 7.9 %collective-permute-done.5.from_below = bf16[384,1536]{1,0:T(8,128)(2,1)S(1)} collective-permute-done((bf16[384,1536]{1,0:T(8,128)(2,1)S(1)}, bf16[384,1536]{1,0:T(8,128)(2,1)S(1)}, u32[]{:S(2)}, u32[]{:S(2)}) %collective-permute-start.5) | collective-permute-done | bytes 1179680 | tf_op jit(solution)/shard_map/ppermute | solution.py:156
  51.2 2.0 %arrive.1 = (f32[384,768]{1,0:T(8,128)S(1)}, f32[384,768]{1,0:T(8,128)S(1)}) custom-call(bf16[384,1536]{1,0:T(8,128)(2,1)S(1)} %collective-permute-done.4.from_above, bf16[384,1536]{1,0:T(8,128)(2,1)S(1)} %collective-permute-done.5.from_below, bf16[2304,768]{1,0:T(8,128)(2,1)S(1)} %get-tuple-element.13.right), custom_call_target="tpu_custom_call" | custom-call | flops 1811939328 | bytes 9437184 | tf_op jit(solution)/shard_map/arrive/pallas_call | solution.py:192
  53.2 1.7 %collective-permute-done.2.centre_above = bf16[384,768]{1,0:T(8,128)(2,1)S(1)} collective-permute-done((bf16[384,768]{1,0:T(8,128)(2,1)S(1)}, bf16[384,768]{1,0:T(8,128)(2,1)S(1)}, u32[]{:S(2)}, u32[]{:S(2)}) %collective-permute-start.2) | collective-permute-done | bytes 589856 | tf_op jit(solution)/shard_map/ppermute | solution.py:168
  54.9 7.6 %collective-permute-done.3.centre_below = bf16[384,768]{1,0:T(8,128)(2,1)S(1)} collective-permute-done((bf16[384,768]{1,0:T(8,128)(2,1)S(1)}, bf16[384,768]{1,0:T(8,128)(2,1)S(1)}, u32[]{:S(2)}, u32[]{:S(2)}) %collective-permute-start.3) | collective-permute-done | bytes 589856 | tf_op jit(solution)/shard_map/ppermute | solution.py:169
  62.5 3.3 %finish.1 = f32[1,1,2,384,384]{4,3,2,1,0:T(8,128)} custom-call(bf16[384,768]{1,0:T(8,128)(2,1)S(1)} %collective-permute-done.2.centre_above, bf16[384,768]{1,0:T(8,128)(2,1)S(1)} %collective-permute-done.3.centre_below, f32[384,768]{1,0:T(8,128)S(1)} %get-tuple-element.14.x_above, f32[384,768]{1,0:T(8,128)S(1)} %get-tuple-element.15.x_below, ...), custom_call_target="tpu_custom_call" | custom-call | flops 1811939328 | bytes 9437184 | tf_op jit(solution)/shard_map/finish/pallas_call | solution.py:200
Async XLA Ops:
  0.0 19.1 %collective-permute-start = (bf16[1,1,2,384,384]{4,3,2,1,0:T(8,128)(2,1)}, bf16[1,1,2,384,384]{4,3,2,1,0:T(8,128)(2,1)S(1)}, u32[]{:S(2)}, u32[]{:S(2)}) collective-permute-start(bf16[1,1,2,384,384]{4,3,2,1,0:T(8,128)(2,1)} %param.8), channel_id=1, source_target_pairs={{0,1},{1,2},{2,3},{3,4},{4,5},{5,6},{6,7},{8,9},{9,10},{10,11},{11... | collective-permute-start | bytes 1769480 | tf_op jit(solution)/shard_map/ppermute | solution.py:136
  1.9 17.2 %collective-permute-start.1 = (bf16[1,1,2,384,384]{4,3,2,1,0:T(8,128)(2,1)}, bf16[1,1,2,384,384]{4,3,2,1,0:T(8,128)(2,1)S(1)}, u32[]{:S(2)}, u32[]{:S(2)}) collective-permute-start(bf16[1,1,2,384,384]{4,3,2,1,0:T(8,128)(2,1)} %param.8), channel_id=1, source_target_pairs={{1,0},{2,1},{3,2},{4,3},{5,4},{6,5},{7,6},{9,8},{10,9},{11,10},{12... | collective-permute-start | bytes 1769480 | tf_op jit(solution)/shard_map/ppermute | solution.py:137
  7.1 1.5 %copy-start = (bf16[1,1,3,2,384,384]{5,4,3,2,1,0:T(8,128)(2,1)S(1)}, bf16[1,1,3,2,384,384]{5,4,3,2,1,0:T(8,128)(2,1)}, u32[]{:S(2)}) copy-start(bf16[1,1,3,2,384,384]{5,4,3,2,1,0:T(8,128)(2,1)} %sigma.3) | copy-start | bytes 5308420
  8.6 0.7 copy-start.2
  12.6 30.8 %collective-permute-start.4 = (bf16[384,1536]{1,0:T(8,128)(2,1)S(1)}, bf16[384,1536]{1,0:T(8,128)(2,1)S(1)}, u32[]{:S(2)}, u32[]{:S(2)}) collective-permute-start(bf16[384,1536]{1,0:T(8,128)(2,1)S(1)} %get-tuple-element.11.low), channel_id=1, source_target_pairs={{8,0},{16,8},{24,16},{32,24},{40,32},{48,40},{56,48},{64,56},{72,6... | collective-permute-start | bytes 3538952 | tf_op jit(solution)/shard_map/ppermute | solution.py:155
  17.0 13.5 %copy-start.1 = (bf16[1,1,3,2,384,384]{5,4,3,2,1,0:T(8,128)(2,1)S(1)}, bf16[1,1,3,2,384,384]{5,4,3,2,1,0:T(8,128)(2,1)}, u32[]{:S(2)}) copy-start(bf16[1,1,3,2,384,384]{5,4,3,2,1,0:T(8,128)(2,1)} %green.3) | copy-start | bytes 5308420
  17.0 34.2 %collective-permute-start.5 = (bf16[384,1536]{1,0:T(8,128)(2,1)S(1)}, bf16[384,1536]{1,0:T(8,128)(2,1)S(1)}, u32[]{:S(2)}, u32[]{:S(2)}) collective-permute-start(bf16[384,1536]{1,0:T(8,128)(2,1)S(1)} %get-tuple-element.12.high), channel_id=1, source_target_pairs={{0,8},{8,16},{16,24},{24,32},{32,40},{40,48},{48,56},{56,64},{64,7... | collective-permute-start | bytes 3538952 | tf_op jit(solution)/shard_map/ppermute | solution.py:156
  21.3 33.6 %collective-permute-start.2 = (bf16[384,768]{1,0:T(8,128)(2,1)S(1)}, bf16[384,768]{1,0:T(8,128)(2,1)S(1)}, u32[]{:S(2)}, u32[]{:S(2)}) collective-permute-start(bf16[384,768]{1,0:T(8,128)(2,1)S(1)} %centre.1), channel_id=1, source_target_pairs={{8,0},{16,8},{24,16},{32,24},{40,32},{48,40},{56,48},{64,56},{72,6... | collective-permute-start | bytes 1769480 | tf_op jit(solution)/shard_map/ppermute | solution.py:168
  28.6 33.9 %collective-permute-start.3 = (bf16[384,768]{1,0:T(8,128)(2,1)S(1)}, bf16[384,768]{1,0:T(8,128)(2,1)S(1)}, u32[]{:S(2)}, u32[]{:S(2)}) collective-permute-start(bf16[384,768]{1,0:T(8,128)(2,1)S(1)} %centre.1), channel_id=1, source_target_pairs={{0,8},{8,16},{16,24},{24,32},{32,40},{40,48},{48,56},{56,64},{64,7... | collective-permute-start | bytes 1769480 | tf_op jit(solution)/shard_map/ppermute | solution.py:169

commit v2 on v1

v2 whole, which is shorter than its diff:
```python
import jax
import jax.numpy as jnp
from jax import lax
from jax.experimental import pallas as pl
from jax.experimental.pallas import tpu as pltpu
from jax.sharding import PartitionSpec as P


F32 = jnp.float32
BF16 = jnp.bfloat16
VMEM_LIMIT = 24 * 1024 * 1024
CHUNKS = 3


def cost(flops, moved):
    return pl.CostEstimate(flops=int(flops), bytes_accessed=int(moved), transcendentals=0)


def dot(left, right):
    return jnp.dot(left, right, preferred_element_type=F32)


def toward():
    return 1 - 2 * lax.rem(lax.axis_index("slab"), 2)


def matches(slab, offset, off, cnt, rng):
    found = []
    for q in range(off.shape[0]):
        live = (off[q, slab] == offset) & (q < cnt[slab])
        found.append((live.astype(jnp.int32), jnp.where(live, rng[q, slab], 0)))
    return found


def masked(block, rows, cols, limit):
    return jnp.where((rows < limit) & (cols < limit), block.astype(F32), 0.0)


def index_grid(first, height, width):
    rows = lax.broadcasted_iota(jnp.int32, (height, width), 0) + first
    cols = lax.broadcasted_iota(jnp.int32, (height, width), 1)
    return rows, cols


def side_kernel(off_in, cnt_in, rng_in, sigma, first, second, off, cnt, rng, held, sems, table_sems):
    slab = lax.axis_index("slab")
    s = toward()
    chunks, slots, _, height, width = held.shape
    tables = [
        pltpu.make_async_copy(src, dst, table_sems.at[n])
        for n, (src, dst) in enumerate(((off_in, off), (cnt_in, cnt), (rng_in, rng)))
    ]
    copies = [
        pltpu.make_async_copy(
            sigma.at[0, 0, :, :, pl.ds(c * height, height), :], held.at[c], sems.at[c]
        )
        for c in range(chunks)
    ]
    for copy in tables + copies:
        copy.start()
    for copy in tables:
        copy.wait()
    wanted = (
        (first, 0, s),
        (first, 1, 2 * s),
        (second, 0, -2 * s),
        (second, 1, -s),
    )
    for c in range(chunks):
        copies[c].wait()
        rows, cols = index_grid(c * height, height, width)
        top = pl.ds(c * height, height)
        for out, slot, offset in wanted:
            found = matches(slab, offset, off, cnt, rng)
            number = sum(live for live, _ in found)
            which = sum(q * live for q, (live, _) in enumerate(found))
            limit = sum(reach for _, reach in found)
            at = [pl.ds((2 * slot + part) * width, width) for part in range(2)]

            @pl.when(number == 0)
            def _():
                for part in range(2):
                    out[top, at[part]] = jnp.zeros((height, width), BF16)

            @pl.when(number == 1)
            def _():
                for part in range(2):
                    out[top, at[part]] = masked(held[c, which, part], rows, cols, limit).astype(BF16)

            @pl.when(number > 1)
            def _():
                for part in range(2):
                    total = jnp.zeros((height, width), F32)
                    for q in range(slots):
                        total = total + masked(held[c, q, part], rows, cols, found[q][1])
                    out[top, at[part]] = total.astype(BF16)


def centre_kernel(off, cnt, rng, sigma, one, two, out):
    slab = lax.axis_index("slab")
    height, width = sigma.shape[-2:]
    rows, cols = index_grid(pl.program_id(0) * height, height, width)
    found = matches(slab, 0, off, cnt, rng)
    for part in range(2):
        mixed = 0.5 * (one[0, 0, part].astype(F32) + two[0, 0, part].astype(F32))
        total = mixed.astype(BF16).astype(F32)
        for q in range(sigma.shape[2]):
            total = total + masked(sigma[0, 0, q, part], rows, cols, found[q][1])
        out[:, part * width : (part + 1) * width] = total.astype(BF16)


def green_kernel(green, right, left):
    width = green.shape[-1]
    s = toward()
    for slot, (o, to) in enumerate(((1 + s, 0), (1, 2), (1 - s, 1))):
        real, imag = green[0, 0, o, 0], green[0, 0, o, 1]
        real_t, imag_t = real.T, imag.T
        at = 2 * slot * width
        right[at : at + width, :width] = real_t
        right[at : at + width, width:] = -imag_t
        right[at + width : at + 2 * width, :width] = imag_t
        right[at + width : at + 2 * width, width:] = real_t
        left[:, 2 * to * width : (2 * to + 1) * width] = real
        left[:, (2 * to + 1) * width : (2 * to + 2) * width] = imag


def spread(x, out, first):
    width = x.shape[1] // 2
    rounded = x.astype(BF16)
    real, imag = rounded[:, :width], rounded[:, width:]
    out[first : first + width, :width] = real
    out[first : first + width, width:] = imag
    out[first + width : first + 2 * width, :width] = -imag
    out[first + width : first + 2 * width, width:] = real


def local_kernel(first, centre, second, right, left, out, held):
    wide = centre.shape[1]
    x = dot(first[:, :wide], right[:wide])
    x = x + dot(centre[...], right[wide : 2 * wide])
    x = x + dot(second[:, wide:], right[2 * wide :])
    spread(x, held, 0)
    out[...] = dot(left[:, 2 * wide :], held[...])


def arrive_kernel(from_first, from_second, right, out_first, out_second):
    wide = out_first.shape[1]
    out_first[...] = dot(from_first[...], right[wide:])
    out_second[...] = dot(from_second[...], right[: 2 * wide])


def finish_kernel(c_first, c_second, x_first, x_second, right, left, partial, out, held, stage, sems):
    wide = c_first.shape[1]
    width = wide // 2
    spread(x_first[...] + dot(c_first[...], right[:wide]), held, 0)
    spread(x_second[...] + dot(c_second[...], right[2 * wide :]), held, wide)
    height = width // CHUNKS
    copies = []
    for c in range(CHUNKS):
        top = pl.ds(c * height, height)
        total = partial[top, :] + dot(left[top, : 2 * wide], held[...])
        stage[0, top, :] = total[:, :width]
        stage[1, top, :] = total[:, width:]
        copies.append(
            pltpu.make_async_copy(stage.at[:, top, :], out.at[0, 0, :, top, :], sems.at[c])
        )
        copies[-1].start()
    for copy in copies:
        copy.wait()


def smem():
    return pl.BlockSpec(memory_space=pltpu.SMEM)


def hbm():
    return pl.BlockSpec(memory_space=pltpu.HBM)


def params():
    return pltpu.CompilerParams(vmem_limit_bytes=VMEM_LIMIT)


def swaps(first, count):
    pairs = []
    for i in range(first, count - 1, 2):
        pairs += [(i, i + 1), (i + 1, i)]
    return pairs


def swap(value, axis, first):
    return lax.ppermute(value, axis, swaps(first, lax.axis_size(axis)))


def in_hbm(value):
    return pltpu.with_memory_space_constraint(value, pltpu.HBM)


def program(green, sigma, phonon, pair_off, pair_count, pair_range):
    width = green.shape[-1]
    wide = 2 * width
    slots = sigma.shape[2]
    tables = (pair_off.T, pair_count, pair_range.T)
    block_bytes = 2 * width * wide
    height = width // CHUNKS

    first, second = pl.pallas_call(
        side_kernel,
        in_specs=[hbm()] * 4,
        out_shape=[jax.ShapeDtypeStruct((width, 2 * wide), BF16)] * 2,
        scratch_shapes=[
            pltpu.SMEM(tables[0].shape, jnp.int32),
            pltpu.SMEM(tables[1].shape, jnp.int32),
            pltpu.SMEM(tables[2].shape, jnp.int32),
            pltpu.VMEM((CHUNKS, slots, 2, height, width), BF16),
            pltpu.SemaphoreType.DMA((CHUNKS,)),
            pltpu.SemaphoreType.DMA((3,)),
        ],
        compiler_params=params(),
        cost_estimate=cost(3e9, 7 * block_bytes),
        name="side",
    )(*[in_hbm(value) for value in (*tables, sigma)])
    from_first = swap(first, "slab", 0)
    from_second = swap(second, "slab", 1)

    one = swap(phonon, "energy", 0)
    two = swap(phonon, "energy", 1)

    sigma_spec = pl.BlockSpec((1, 1, slots, 2, height, width), lambda c: (0, 0, 0, 0, c, 0))
    phonon_spec = pl.BlockSpec((1, 1, 2, height, width), lambda c: (0, 0, 0, c, 0))
    centre = pl.pallas_call(
        centre_kernel,
        grid=(CHUNKS,),
        in_specs=[smem(), smem(), smem(), sigma_spec, phonon_spec, phonon_spec],
        out_specs=pl.BlockSpec((height, wide), lambda c: (c, 0)),
        out_shape=jax.ShapeDtypeStruct((width, wide), BF16),
        compiler_params=params(),
        cost_estimate=cost(3e9, 6 * block_bytes),
        name="centre",
    )(*[in_hbm(value) for value in (*tables, sigma)], one, two)
    c_first = swap(centre, "slab", 0)
    c_second = swap(centre, "slab", 1)

    right, left = pl.pallas_call(
        green_kernel,
        out_shape=[
            jax.ShapeDtypeStruct((3 * wide, wide), BF16),
            jax.ShapeDtypeStruct((width, 3 * wide), BF16),
        ],
        compiler_params=params(),
        cost_estimate=cost(4e9, 12 * block_bytes),
        name="green",
    )(green)

    square = jax.ShapeDtypeStruct((width, wide), F32)
    partial = pl.pallas_call(
        local_kernel,
        out_shape=square,
        scratch_shapes=[pltpu.VMEM((wide, wide), BF16)],
        compiler_params=params(),
        cost_estimate=cost(2 * width * wide * 4 * wide, 16 * block_bytes),
        name="local",
    )(first, centre, second, right, left)

    x_first, x_second = pl.pallas_call(
        arrive_kernel,
        out_shape=[square, square],
        compiler_params=params(),
        cost_estimate=cost(2 * width * wide * 4 * wide, 16 * block_bytes),
        name="arrive",
    )(from_first, from_second, right)

    return pl.pallas_call(
        finish_kernel,
        out_specs=hbm(),
        out_shape=jax.ShapeDtypeStruct((1, 1, 2, width, width), F32),
        scratch_shapes=[
            pltpu.VMEM((2 * wide, wide), BF16),
            pltpu.VMEM((2, width, width), F32),
            pltpu.SemaphoreType.DMA((CHUNKS,)),
        ],
        compiler_params=params(),
        cost_estimate=cost(2 * width * wide * 4 * wide, 16 * block_bytes),
        name="finish",
    )(c_first, c_second, x_first, x_second, right, left, partial)


def solution(mesh):
    in_specs = (
        P("energy", "slab", None, None, None, None),
        P("energy", "slab", None, None, None, None),
        P("energy", "slab", None, None, None),
        P(),
        P(),
        P(),
    )
    out_specs = P("energy", "slab", None, None, None)
    return jax.shard_map(program, mesh=mesh, in_specs=in_specs, out_specs=out_specs, check_vma=False)
```

time: 66.1 us -> 55.6 us (0.84)
  starting transfers between devices: 21.2 us -> 12.8 us
  local copies, waits for them, and re-layouts: 3.66 us -> 0.01 us
  waiting for transfers between devices: 26.5 us -> 29.2 us
  Pallas kernels: 14.2 us -> 13.3 us
    ppermute x6, starting transfers between devices: 21.2 us -> 12.8 us  [swap(): return lax.ppermute(value, axis, swaps(first, lax.axis_size(axis)))]
    unnamed x8 -> x2, local copies, waits for them, and re-layouts: 3.66 us -> 0.01 us
    ppermute x6, waiting for transfers between devices: 26.5 us -> 29.2 us  [swap(): return lax.ppermute(value, axis, swaps(first, lax.axis_size(axis)))]
    pallas_call x6, Pallas kernels: 14.2 us -> 13.3 us  [the longest x1 2.95 us: program(): pl.pallas_call(finish_kernel, out_specs=hbm(), out_shape=jax.ShapeDtypeSt...]
  transfers between devices with their start and end apart: 6 -> 6, of which waited for: 4 -> 5; matrix products, arithmetic and copies ran while one was open for 2% -> 0% of each run, Pallas kernels for 17% -> 19%
where the time goes in v2:
time: 55.6 us; the launch traced here: 55.4 us
  waiting for transfers between devices  29.2 us (53%)
  Pallas kernels  13.3 us (24%)
  starting transfers between devices  12.8 us (23%)
    ppermute x6, waiting for transfers between devices, swap(): return lax.ppermute(value, axis, swaps(first, lax.axis_size(axis)))  29.2 us
    ppermute x6, starting transfers between devices, swap(): return lax.ppermute(value, axis, swaps(first, lax.axis_size(axis)))  12.8 us
    pallas_call x1, Pallas kernels, program(): pl.pallas_call(finish_kernel, out_specs=hbm(), out_shape=jax.ShapeDtypeSt...  2.95 us
    pallas_call x1, Pallas kernels, program(): pl.pallas_call(local_kernel, out_shape=square, scratch_shapes=[pltpu.VMEM...  2.85 us
    pallas_call x1, Pallas kernels, program(): pl.pallas_call(centre_kernel, grid=(CHUNKS,), in_specs=[smem(), smem(), s...  2.73 us
    pallas_call x1, Pallas kernels, program(): pl.pallas_call(side_kernel, in_specs=[hbm()] * 4, out_shape=[jax.ShapeDty...  2.16 us
    pallas_call x1, Pallas kernels, program(): pl.pallas_call(arrive_kernel, out_shape=[square, square], compiler_params...  1.98 us
  transfers between devices with their start and end apart: 6, of which 5 were waited for; matrix products, arithmetic and copies ran while one was open for 0% of the time, Pallas kernels for 19%

profile of v2, /device:TPU:130, one launch (start us, length us, event | category | flops | bytes accessed | tf_op | source)
XLA Modules:
  0.0 55.4 jit_solution(5538488455479344141)
XLA Ops:
  0.0 0.0 collective-permute-start
  0.0 2.5 %collective-permute-start.1 = (bf16[1,1,2,384,384]{4,3,2,1,0:T(8,128)(2,1)}, bf16[1,1,2,384,384]{4,3,2,1,0:T(8,128)(2,1)S(1)}, u32[]{:S(2)}, u32[]{:S(2)}) collective-permute-start(bf16[1,1,2,384,384]{4,3,2,1,0:T(8,128)(2,1)} %param.8), channel_id=1, source_target_pairs={{1,2},{2,1},{3,4},{4,3},{5,6},{6,5},{9,10},{10,9},{11,12},{12,11},... | collective-permute-start | bytes 1769480 | tf_op jit(solution)/shard_map/ppermute | solution.py:192
  2.6 2.2 %side.1 = (bf16[384,1536]{1,0:T(8,128)(2,1)S(1)}, bf16[384,1536]{1,0:T(8,128)(2,1)S(1)}) custom-call(s32[3,32]{1,0:T(4,128)} %bitcast.2, s32[32]{0:T(128)} %cnt_in.1, s32[3,32]{1,0:T(4,128)} %bitcast.4, bf16[1,1,3,2,384,384]{5,4,3,2,1,0:T(8,128)(2,1)} %sigma.3), custom_call_target="tpu_custom_call" | custom-call | flops 3000000000 | bytes 4128768 | tf_op jit(solution)/shard_map/side/pallas_call | solution.py:207
  4.7 1.2 %collective-permute-start.4 = (bf16[384,1536]{1,0:T(8,128)(2,1)S(1)}, bf16[384,1536]{1,0:T(8,128)(2,1)S(1)}, u32[]{:S(2)}, u32[]{:S(2)}) collective-permute-start(bf16[384,1536]{1,0:T(8,128)(2,1)S(1)} %get-tuple-element.11.first), channel_id=1, source_target_pairs={{0,8},{8,0},{16,24},{24,16},{32,40},{40,32},{48,56},{56,48},{64,72... | collective-permute-start | bytes 3538952 | tf_op jit(solution)/shard_map/ppermute | solution.py:192
  5.9 0.0 copy-start
  5.9 3.8 %collective-permute-start.5 = (bf16[384,1536]{1,0:T(8,128)(2,1)S(1)}, bf16[384,1536]{1,0:T(8,128)(2,1)S(1)}, u32[]{:S(2)}, u32[]{:S(2)}) collective-permute-start(bf16[384,1536]{1,0:T(8,128)(2,1)S(1)} %get-tuple-element.12.second), channel_id=1, source_target_pairs={{8,16},{16,8},{24,32},{32,24},{40,48},{48,40},{56,64},{64,56},{72,... | collective-permute-start | bytes 3538952 | tf_op jit(solution)/shard_map/ppermute | solution.py:192
  9.7 0.0 collective-permute-done.one
  9.7 1.7 %collective-permute-done.1.two = bf16[1,1,2,384,384]{4,3,2,1,0:T(8,128)(2,1)S(1)} collective-permute-done((bf16[1,1,2,384,384]{4,3,2,1,0:T(8,128)(2,1)}, bf16[1,1,2,384,384]{4,3,2,1,0:T(8,128)(2,1)S(1)}, u32[]{:S(2)}, u32[]{:S(2)}) %collective-permute-start.1) | collective-permute-done | bytes 589856 | tf_op jit(solution)/shard_map/ppermute | solution.py:192
  11.4 2.7 %centre.1 = bf16[384,768]{1,0:T(8,128)(2,1)S(1)} custom-call(s32[3,32]{1,0:T(4,128)} %bitcast.3, s32[32]{0:T(128)} %cnt_in.1, s32[3,32]{1,0:T(4,128)} %bitcast.5, bf16[1,1,3,2,384,384]{5,4,3,2,1,0:T(8,128)(2,1)} %sigma.3, bf16[1,1,2,384,384]{4,3,2,1,0:T(8,128)(2,1)S(1)} %collective-permute-done.one, bf16[1,1,2,384,384]{4,3,2,1,0:T(8,128)(2,1)S(1)} %collective-permute-done.1.two), custom_call_target="tpu_custom_call" | custom-call | flops 3000000000 | bytes 3538944 | tf_op jit(solution)/shard_map/centre/pallas_call | solution.py:231
  14.1 1.7 %collective-permute-start.2 = (bf16[384,768]{1,0:T(8,128)(2,1)S(1)}, bf16[384,768]{1,0:T(8,128)(2,1)S(1)}, u32[]{:S(2)}, u32[]{:S(2)}) collective-permute-start(bf16[384,768]{1,0:T(8,128)(2,1)S(1)} %centre.1), channel_id=1, source_target_pairs={{0,8},{8,0},{16,24},{24,16},{32,40},{40,32},{48,56},{56,48},{64,72... | collective-permute-start | bytes 1769480 | tf_op jit(solution)/shard_map/ppermute | solution.py:192
  15.8 3.6 %collective-permute-start.3 = (bf16[384,768]{1,0:T(8,128)(2,1)S(1)}, bf16[384,768]{1,0:T(8,128)(2,1)S(1)}, u32[]{:S(2)}, u32[]{:S(2)}) collective-permute-start(bf16[384,768]{1,0:T(8,128)(2,1)S(1)} %centre.1), channel_id=1, source_target_pairs={{8,16},{16,8},{24,32},{32,24},{40,48},{48,40},{56,64},{64,56},{72,... | collective-permute-start | bytes 1769480 | tf_op jit(solution)/shard_map/ppermute | solution.py:192
  19.4 0.0 copy-done
  19.4 0.6 %green.2 = (bf16[2304,768]{1,0:T(8,128)(2,1)S(1)}, bf16[384,2304]{1,0:T(8,128)(2,1)S(1)}) custom-call(bf16[1,1,3,2,384,384]{5,4,3,2,1,0:T(8,128)(2,1)S(1)} %copy-done), custom_call_target="tpu_custom_call" | custom-call | flops 4000000000 | bytes 7077888 | tf_op jit(solution)/shard_map/green/pallas_call | solution.py:244
  20.1 2.8 %local.1.partial = f32[384,768]{1,0:T(8,128)S(1)} custom-call(bf16[384,1536]{1,0:T(8,128)(2,1)S(1)} %get-tuple-element.11.first, bf16[384,768]{1,0:T(8,128)(2,1)S(1)} %centre.1, bf16[384,1536]{1,0:T(8,128)(2,1)S(1)} %get-tuple-element.12.second, bf16[2304,768]{1,0:T(8,128)(2,1)S(1)} %get-tuple-element.13.right, bf16[384,2304]{1,0:T(8,128)(2,1)S(1)} %get-tuple-element.16.left), custom_call_target="tpu_custom_call" | custom-call | flops 1811939328 | bytes 9437184 | tf_op jit(solution)/shard_map/local/pallas_call | solution.py:256
  22.9 10.7 %collective-permute-done.4.from_first = bf16[384,1536]{1,0:T(8,128)(2,1)S(1)} collective-permute-done((bf16[384,1536]{1,0:T(8,128)(2,1)S(1)}, bf16[384,1536]{1,0:T(8,128)(2,1)S(1)}, u32[]{:S(2)}, u32[]{:S(2)}) %collective-permute-start.4) | collective-permute-done | bytes 1179680 | tf_op jit(solution)/shard_map/ppermute | solution.py:192
  33.7 6.4 %collective-permute-done.5.from_second = bf16[384,1536]{1,0:T(8,128)(2,1)S(1)} collective-permute-done((bf16[384,1536]{1,0:T(8,128)(2,1)S(1)}, bf16[384,1536]{1,0:T(8,128)(2,1)S(1)}, u32[]{:S(2)}, u32[]{:S(2)}) %collective-permute-start.5) | collective-permute-done | bytes 1179680 | tf_op jit(solution)/shard_map/ppermute | solution.py:192
  40.1 2.0 %arrive.1 = (f32[384,768]{1,0:T(8,128)S(1)}, f32[384,768]{1,0:T(8,128)S(1)}) custom-call(bf16[384,1536]{1,0:T(8,128)(2,1)S(1)} %collective-permute-done.4.from_first, bf16[384,1536]{1,0:T(8,128)(2,1)S(1)} %collective-permute-done.5.from_second, bf16[2304,768]{1,0:T(8,128)(2,1)S(1)} %get-tuple-element.13.right), custom_call_target="tpu_custom_call" | custom-call | flops 1811939328 | bytes 9437184 | tf_op jit(solution)/shard_map/arrive/pallas_call | solution.py:265
  42.1 4.2 %collective-permute-done.2.c_first = bf16[384,768]{1,0:T(8,128)(2,1)S(1)} collective-permute-done((bf16[384,768]{1,0:T(8,128)(2,1)S(1)}, bf16[384,768]{1,0:T(8,128)(2,1)S(1)}, u32[]{:S(2)}, u32[]{:S(2)}) %collective-permute-start.2) | collective-permute-done | bytes 589856 | tf_op jit(solution)/shard_map/ppermute | solution.py:192
  46.3 6.2 %collective-permute-done.3.c_second = bf16[384,768]{1,0:T(8,128)(2,1)S(1)} collective-permute-done((bf16[384,768]{1,0:T(8,128)(2,1)S(1)}, bf16[384,768]{1,0:T(8,128)(2,1)S(1)}, u32[]{:S(2)}, u32[]{:S(2)}) %collective-permute-start.3) | collective-permute-done | bytes 589856 | tf_op jit(solution)/shard_map/ppermute | solution.py:192
  52.4 2.9 %finish.1 = f32[1,1,2,384,384]{4,3,2,1,0:T(8,128)} custom-call(bf16[384,768]{1,0:T(8,128)(2,1)S(1)} %collective-permute-done.2.c_first, bf16[384,768]{1,0:T(8,128)(2,1)S(1)} %collective-permute-done.3.c_second, f32[384,768]{1,0:T(8,128)S(1)} %get-tuple-element.14.x_first, f32[384,768]{1,0:T(8,128)S(1)} %get-tuple-element.15.x_second, ...), custom_call_target="tpu_custom_call" | custom-call | flops 1811939328 | bytes 9437184 | tf_op jit(solution)/shard_map/finish/pallas_call | solution.py:273
Async XLA Ops:
  0.0 9.7 %collective-permute-start = (bf16[1,1,2,384,384]{4,3,2,1,0:T(8,128)(2,1)}, bf16[1,1,2,384,384]{4,3,2,1,0:T(8,128)(2,1)S(1)}, u32[]{:S(2)}, u32[]{:S(2)}) collective-permute-start(bf16[1,1,2,384,384]{4,3,2,1,0:T(8,128)(2,1)} %param.8), channel_id=1, source_target_pairs={{0,1},{1,0},{2,3},{3,2},{4,5},{5,4},{6,7},{7,6},{8,9},{9,8},{10,11... | collective-permute-start | bytes 1769480 | tf_op jit(solution)/shard_map/ppermute | solution.py:192
  0.0 11.4 %collective-permute-start.1 = (bf16[1,1,2,384,384]{4,3,2,1,0:T(8,128)(2,1)}, bf16[1,1,2,384,384]{4,3,2,1,0:T(8,128)(2,1)S(1)}, u32[]{:S(2)}, u32[]{:S(2)}) collective-permute-start(bf16[1,1,2,384,384]{4,3,2,1,0:T(8,128)(2,1)} %param.8), channel_id=1, source_target_pairs={{1,2},{2,1},{3,4},{4,3},{5,6},{6,5},{9,10},{10,9},{11,12},{12,11},... | collective-permute-start | bytes 1769480 | tf_op jit(solution)/shard_map/ppermute | solution.py:192
  4.7 28.9 %collective-permute-start.4 = (bf16[384,1536]{1,0:T(8,128)(2,1)S(1)}, bf16[384,1536]{1,0:T(8,128)(2,1)S(1)}, u32[]{:S(2)}, u32[]{:S(2)}) collective-permute-start(bf16[384,1536]{1,0:T(8,128)(2,1)S(1)} %get-tuple-element.11.first), channel_id=1, source_target_pairs={{0,8},{8,0},{16,24},{24,16},{32,40},{40,32},{48,56},{56,48},{64,72... | collective-permute-start | bytes 3538952 | tf_op jit(solution)/shard_map/ppermute | solution.py:192
  5.9 13.5 %copy-start = (bf16[1,1,3,2,384,384]{5,4,3,2,1,0:T(8,128)(2,1)S(1)}, bf16[1,1,3,2,384,384]{5,4,3,2,1,0:T(8,128)(2,1)}, u32[]{:S(2)}) copy-start(bf16[1,1,3,2,384,384]{5,4,3,2,1,0:T(8,128)(2,1)} %green.3) | copy-start | bytes 5308420
  5.9 34.2 %collective-permute-start.5 = (bf16[384,1536]{1,0:T(8,128)(2,1)S(1)}, bf16[384,1536]{1,0:T(8,128)(2,1)S(1)}, u32[]{:S(2)}, u32[]{:S(2)}) collective-permute-start(bf16[384,1536]{1,0:T(8,128)(2,1)S(1)} %get-tuple-element.12.second), channel_id=1, source_target_pairs={{8,16},{16,8},{24,32},{32,24},{40,48},{48,40},{56,64},{64,56},{72,... | collective-permute-start | bytes 3538952 | tf_op jit(solution)/shard_map/ppermute | solution.py:192
  14.1 32.1 %collective-permute-start.2 = (bf16[384,768]{1,0:T(8,128)(2,1)S(1)}, bf16[384,768]{1,0:T(8,128)(2,1)S(1)}, u32[]{:S(2)}, u32[]{:S(2)}) collective-permute-start(bf16[384,768]{1,0:T(8,128)(2,1)S(1)} %centre.1), channel_id=1, source_target_pairs={{0,8},{8,0},{16,24},{24,16},{32,40},{40,32},{48,56},{56,48},{64,72... | collective-permute-start | bytes 1769480 | tf_op jit(solution)/shard_map/ppermute | solution.py:192
  15.8 36.6 %collective-permute-start.3 = (bf16[384,768]{1,0:T(8,128)(2,1)S(1)}, bf16[384,768]{1,0:T(8,128)(2,1)S(1)}, u32[]{:S(2)}, u32[]{:S(2)}) collective-permute-start(bf16[384,768]{1,0:T(8,128)(2,1)S(1)} %centre.1), channel_id=1, source_target_pairs={{8,16},{16,8},{24,32},{32,24},{40,48},{48,40},{56,64},{64,56},{72,... | collective-permute-start | bytes 1769480 | tf_op jit(solution)/shard_map/ppermute | solution.py:192

commit v3 on v2

--- a/solution.py
+++ b/solution.py
@@ -10,6 +10,7 @@
 BF16 = jnp.bfloat16
 VMEM_LIMIT = 24 * 1024 * 1024
 CHUNKS = 3
+SPLIT = 256
 
 
 def cost(flops, moved):
@@ -96,23 +97,33 @@
                     out[top, at[part]] = total.astype(BF16)
 
 
-def centre_kernel(off, cnt, rng, sigma, one, two, out):
+def centre_kernel(off, cnt, rng, sigma, one, two, early, late):
     slab = lax.axis_index("slab")
+    step = pl.program_id(0)
     height, width = sigma.shape[-2:]
-    rows, cols = index_grid(pl.program_id(0) * height, height, width)
+    rows, cols = index_grid(step * height, height, width)
     found = matches(slab, 0, off, cnt, rng)
     for part in range(2):
         mixed = 0.5 * (one[0, 0, part].astype(F32) + two[0, 0, part].astype(F32))
         total = mixed.astype(BF16).astype(F32)
         for q in range(sigma.shape[2]):
             total = total + masked(sigma[0, 0, q, part], rows, cols, found[q][1])
-        out[:, part * width : (part + 1) * width] = total.astype(BF16)
-
-
-def green_kernel(green, right, left):
+        at = pl.ds(part * width, width)
+
+        @pl.when(step < SPLIT // height)
+        def _():
+            early[pl.ds(pl.multiple_of(step * height, height), height), at] = total.astype(BF16)
+
+        @pl.when(step >= SPLIT // height)
+        def _():
+            below = pl.multiple_of(step * height - SPLIT, height)
+            late[pl.ds(below, height), at] = total.astype(BF16)
+
+
+def green_kernel(green, right, left, left_early, left_late):
     width = green.shape[-1]
     s = toward()
-    for slot, (o, to) in enumerate(((1 + s, 0), (1, 2), (1 - s, 1))):
+    for slot, o in enumerate((1 + s, 1, 1 - s)):
         real, imag = green[0, 0, o, 0], green[0, 0, o, 1]
         real_t, imag_t = real.T, imag.T
         at = 2 * slot * width
@@ -120,27 +131,34 @@
         right[at : at + width, width:] = -imag_t
         right[at + width : at + 2 * width, :width] = imag_t
         right[at + width : at + 2 * width, width:] = real_t
-        left[:, 2 * to * width : (2 * to + 1) * width] = real
-        left[:, (2 * to + 1) * width : (2 * to + 2) * width] = imag
+        if slot == 1:
+            left[:, :width] = real
+            left[:, width:] = imag
+        else:
+            for out, first, last in ((left_early, 0, SPLIT), (left_late, SPLIT, width)):
+                height = last - first
+                to = slot * height
+                out[:, to : to + height] = real[:, first:last]
+                out[:, to + height : to + 2 * height] = imag[:, first:last]
 
 
 def spread(x, out, first):
-    width = x.shape[1] // 2
+    height, width = x.shape[0], x.shape[1] // 2
     rounded = x.astype(BF16)
     real, imag = rounded[:, :width], rounded[:, width:]
-    out[first : first + width, :width] = real
-    out[first : first + width, width:] = imag
-    out[first + width : first + 2 * width, :width] = -imag
-    out[first + width : first + 2 * width, width:] = real
-
-
-def local_kernel(first, centre, second, right, left, out, held):
-    wide = centre.shape[1]
-    x = dot(first[:, :wide], right[:wide])
-    x = x + dot(centre[...], right[wide : 2 * wide])
-    x = x + dot(second[:, wide:], right[2 * wide :])
+    out[first : first + height, :width] = real
+    out[first : first + height, width:] = imag
+    out[first + height : first + 2 * height, :width] = -imag
+    out[first + height : first + 2 * height, width:] = real
+
+
+def local_kernel(first, early, late, second, right, left, out, held):
+    wide = early.shape[1]
+    x = dot(first[:, :wide], right[:wide]) + dot(second[:, wide:], right[2 * wide :])
+    middle = right[wide : 2 * wide]
+    x = x + jnp.concatenate([dot(early[...], middle), dot(late[...], middle)], axis=0)
     spread(x, held, 0)
-    out[...] = dot(left[:, 2 * wide :], held[...])
+    out[...] = dot(left[...], held[...])
 
 
 def arrive_kernel(from_first, from_second, right, out_first, out_second):
@@ -149,16 +167,26 @@
     out_second[...] = dot(from_second[...], right[: 2 * wide])
 
 
-def finish_kernel(c_first, c_second, x_first, x_second, right, left, partial, out, held, stage, sems):
-    wide = c_first.shape[1]
-    width = wide // 2
-    spread(x_first[...] + dot(c_first[...], right[:wide]), held, 0)
-    spread(x_second[...] + dot(c_second[...], right[2 * wide :]), held, wide)
+def fold(c_first, c_second, x_first, x_second, right, held, first):
+    height, wide = c_first.shape
+    top = slice(first, first + height)
+    spread(x_first[top, :] + dot(c_first[...], right[:wide]), held, 0)
+    spread(x_second[top, :] + dot(c_second[...], right[2 * wide :]), held, 2 * height)
+
+
+def early_kernel(c_first, c_second, x_first, x_second, right, left, partial, out, held):
+    fold(c_first, c_second, x_first, x_second, right, held, 0)
+    out[...] = partial[...] + dot(left[...], held[...])
+
+
+def late_kernel(c_first, c_second, x_first, x_second, right, left, partial, out, held, stage, sems):
+    width = stage.shape[-1]
+    fold(c_first, c_second, x_first, x_second, right, held, SPLIT)
     height = width // CHUNKS
     copies = []
     for c in range(CHUNKS):
         top = pl.ds(c * height, height)
-        total = partial[top, :] + dot(left[top, : 2 * wide], held[...])
+        total = partial[top, :] + dot(left[top, :], held[...])
         stage[0, top, :] = total[:, :width]
         stage[1, top, :] = total[:, width:]
         copies.append(
@@ -228,61 +256,79 @@
 
     sigma_spec = pl.BlockSpec((1, 1, slots, 2, height, width), lambda c: (0, 0, 0, 0, c, 0))
     phonon_spec = pl.BlockSpec((1, 1, 2, height, width), lambda c: (0, 0, 0, c, 0))
-    centre = pl.pallas_call(
+    whole = lambda rows: pl.BlockSpec((rows, wide), lambda c: (0, 0))
+    early, late = pl.pallas_call(
         centre_kernel,
         grid=(CHUNKS,),
         in_specs=[smem(), smem(), smem(), sigma_spec, phonon_spec, phonon_spec],
-        out_specs=pl.BlockSpec((height, wide), lambda c: (c, 0)),
-        out_shape=jax.ShapeDtypeStruct((width, wide), BF16),
+        out_specs=[whole(SPLIT), whole(width - SPLIT)],
+        out_shape=[
+            jax.ShapeDtypeStruct((SPLIT, wide), BF16),
+            jax.ShapeDtypeStruct((width - SPLIT, wide), BF16),
+        ],
         compiler_params=params(),
         cost_estimate=cost(3e9, 6 * block_bytes),
         name="centre",
     )(*[in_hbm(value) for value in (*tables, sigma)], one, two)
-    c_first = swap(centre, "slab", 0)
-    c_second = swap(centre, "slab", 1)
-
-    right, left = pl.pallas_call(
+    early_second = swap(early, "slab", 1)
+    early_first = swap(early, "slab", 0)
+    late_second = swap(late, "slab", 1)
+    late_first = swap(late, "slab", 0)
+
+    right, left, left_early, left_late = pl.pallas_call(
         green_kernel,
         out_shape=[
             jax.ShapeDtypeStruct((3 * wide, wide), BF16),
-            jax.ShapeDtypeStruct((width, 3 * wide), BF16),
+            jax.ShapeDtypeStruct((width, wide), BF16),
+            jax.ShapeDtypeStruct((width, 4 * SPLIT), BF16),
+            jax.ShapeDtypeStruct((width, 4 * (width - SPLIT)), BF16),
         ],
         compiler_params=params(),
         cost_estimate=cost(4e9, 12 * block_bytes),
         name="green",
-    )(green)
+    )(in_hbm(green))
 
     square = jax.ShapeDtypeStruct((width, wide), F32)
+    unit = 2 * width * wide * wide
     partial = pl.pallas_call(
         local_kernel,
         out_shape=square,
         scratch_shapes=[pltpu.VMEM((wide, wide), BF16)],
         compiler_params=params(),
-        cost_estimate=cost(2 * width * wide * 4 * wide, 16 * block_bytes),
+        cost_estimate=cost(4 * unit, 16 * block_bytes),
         name="local",
-    )(first, centre, second, right, left)
+    )(first, early, late, second, right, left)
 
     x_first, x_second = pl.pallas_call(
         arrive_kernel,
         out_shape=[square, square],
         compiler_params=params(),
-        cost_estimate=cost(2 * width * wide * 4 * wide, 16 * block_bytes),
+        cost_estimate=cost(4 * unit, 16 * block_bytes),
         name="arrive",
     )(from_first, from_second, right)
 
+    partial = pl.pallas_call(
+        early_kernel,
+        out_shape=square,
+        scratch_shapes=[pltpu.VMEM((4 * SPLIT, wide), BF16)],
+        compiler_params=params(),
+        cost_estimate=cost(3 * unit, 16 * block_bytes),
+        name="early",
+    )(early_first, early_second, x_first, x_second, right, left_early, partial)
+
     return pl.pallas_call(
-        finish_kernel,
+        late_kernel,
         out_specs=hbm(),
         out_shape=jax.ShapeDtypeStruct((1, 1, 2, width, width), F32),
         scratch_shapes=[
-            pltpu.VMEM((2 * wide, wide), BF16),
+            pltpu.VMEM((4 * (width - SPLIT), wide), BF16),
             pltpu.VMEM((2, width, width), F32),
             pltpu.SemaphoreType.DMA((CHUNKS,)),
         ],
         compiler_params=params(),
-        cost_estimate=cost(2 * width * wide * 4 * wide, 16 * block_bytes),
-        name="finish",
-    )(c_first, c_second, x_first, x_second, right, left, partial)
+        cost_estimate=cost(2 * unit, 16 * block_bytes),
+        name="late",
+    )(late_first, late_second, x_first, x_second, right, left_late, partial)
 
 
 def solution(mesh):

time: 55.6 us -> 54.5 us (0.980)
  waiting for transfers between devices: 29.2 us -> 20.8 us
  starting transfers between devices: 12.8 us -> 18.1 us
  Pallas kernels: 13.3 us -> 15.1 us
    ppermute x6 -> x8, waiting for transfers between devices: 29.2 us -> 20.8 us  [swap(): return lax.ppermute(value, axis, swaps(first, lax.axis_size(axis)))]
    ppermute x6 -> x8, starting transfers between devices: 12.8 us -> 18.1 us  [swap(): return lax.ppermute(value, axis, swaps(first, lax.axis_size(axis)))]
    pallas_call x1, Pallas kernels: 0.63 us -> 2.12 us  [program(): pl.pallas_call(green_kernel, out_shape=[jax.ShapeDtypeStruct((3 * wide, w...]
    pallas_call x1 -> x2, Pallas kernels: 2.95 us -> 3.18 us  [the longest x1 1.78 us: program(): pl.pallas_call(late_kernel, out_specs=hbm(), out_shape=jax.ShapeDtypeStru...]
  transfers between devices with their start and end apart: 6 -> 8, of which waited for: 5 -> 6; matrix products, arithmetic and copies ran while one was open for 0% -> 0% of each run, Pallas kernels for 19% -> 25%
where the time goes in v3:
time: 54.5 us; the launch traced here: 54.2 us
  waiting for transfers between devices  20.8 us (38%)
  starting transfers between devices  18.1 us (33%)
  Pallas kernels  15.1 us (28%)
    ppermute x8, waiting for transfers between devices, swap(): return lax.ppermute(value, axis, swaps(first, lax.axis_size(axis)))  20.8 us
    ppermute x8, starting transfers between devices, swap(): return lax.ppermute(value, axis, swaps(first, lax.axis_size(axis)))  18.1 us
    pallas_call x1, Pallas kernels, program(): pl.pallas_call(local_kernel, out_shape=square, scratch_shapes=[pltpu.VMEM...  2.84 us
    pallas_call x1, Pallas kernels, program(): pl.pallas_call(centre_kernel, grid=(CHUNKS,), in_specs=[smem(), smem(), s...  2.82 us
    pallas_call x1, Pallas kernels, program(): pl.pallas_call(side_kernel, in_specs=[hbm()] * 4, out_shape=[jax.ShapeDty...  2.16 us
    pallas_call x1, Pallas kernels, program(): pl.pallas_call(green_kernel, out_shape=[jax.ShapeDtypeStruct((3 * wide, w...  2.12 us
    pallas_call x1, Pallas kernels, program(): pl.pallas_call(arrive_kernel, out_shape=[square, square], compiler_params...  1.98 us
    pallas_call x1, Pallas kernels, program(): pl.pallas_call(late_kernel, out_specs=hbm(), out_shape=jax.ShapeDtypeStru...  1.78 us
  transfers between devices with their start and end apart: 8, of which 6 were waited for; matrix products, arithmetic and copies ran while one was open for 0% of the time, Pallas kernels for 25%

profile of v3, /device:TPU:130, one launch (start us, length us, event | category | flops | bytes accessed | tf_op | source)
XLA Modules:
  0.0 54.2 jit_solution(187236411583000933)
XLA Ops:
  0.0 0.0 collective-permute-start
  0.0 2.5 %collective-permute-start.1 = (bf16[1,1,2,384,384]{4,3,2,1,0:T(8,128)(2,1)}, bf16[1,1,2,384,384]{4,3,2,1,0:T(8,128)(2,1)S(1)}, u32[]{:S(2)}, u32[]{:S(2)}) collective-permute-start(bf16[1,1,2,384,384]{4,3,2,1,0:T(8,128)(2,1)} %param.8), channel_id=1, source_target_pairs={{1,2},{2,1},{3,4},{4,3},{5,6},{6,5},{9,10},{10,9},{11,12},{12,11},... | collective-permute-start | bytes 1769480 | tf_op jit(solution)/shard_map/ppermute | solution.py:220
  2.6 2.2 %side.1 = (bf16[384,1536]{1,0:T(8,128)(2,1)S(1)}, bf16[384,1536]{1,0:T(8,128)(2,1)S(1)}) custom-call(s32[3,32]{1,0:T(4,128)} %bitcast.2, s32[32]{0:T(128)} %cnt_in.1, s32[3,32]{1,0:T(4,128)} %bitcast.4, bf16[1,1,3,2,384,384]{5,4,3,2,1,0:T(8,128)(2,1)} %sigma.3), custom_call_target="tpu_custom_call" | custom-call | flops 3000000000 | bytes 4128768 | tf_op jit(solution)/shard_map/side/pallas_call | solution.py:235
  4.7 1.2 %collective-permute-start.4 = (bf16[384,1536]{1,0:T(8,128)(2,1)S(1)}, bf16[384,1536]{1,0:T(8,128)(2,1)S(1)}, u32[]{:S(2)}, u32[]{:S(2)}) collective-permute-start(bf16[384,1536]{1,0:T(8,128)(2,1)S(1)} %get-tuple-element.16.first), channel_id=1, source_target_pairs={{0,8},{8,0},{16,24},{24,16},{32,40},{40,32},{48,56},{56,48},{64,72... | collective-permute-start | bytes 3538952 | tf_op jit(solution)/shard_map/ppermute | solution.py:220
  5.9 3.6 %collective-permute-start.5 = (bf16[384,1536]{1,0:T(8,128)(2,1)S(1)}, bf16[384,1536]{1,0:T(8,128)(2,1)S(1)}, u32[]{:S(2)}, u32[]{:S(2)}) collective-permute-start(bf16[384,1536]{1,0:T(8,128)(2,1)S(1)} %get-tuple-element.17.second), channel_id=1, source_target_pairs={{8,16},{16,8},{24,32},{32,24},{40,48},{48,40},{56,64},{64,56},{72,... | collective-permute-start | bytes 3538952 | tf_op jit(solution)/shard_map/ppermute | solution.py:220
  9.5 0.0 collective-permute-done.one
  9.6 1.9 %collective-permute-done.1.two = bf16[1,1,2,384,384]{4,3,2,1,0:T(8,128)(2,1)S(1)} collective-permute-done((bf16[1,1,2,384,384]{4,3,2,1,0:T(8,128)(2,1)}, bf16[1,1,2,384,384]{4,3,2,1,0:T(8,128)(2,1)S(1)}, u32[]{:S(2)}, u32[]{:S(2)}) %collective-permute-start.1) | collective-permute-done | bytes 589856 | tf_op jit(solution)/shard_map/ppermute | solution.py:220
  11.4 2.8 %centre.1 = (bf16[256,768]{1,0:T(8,128)(2,1)S(1)}, bf16[128,768]{1,0:T(8,128)(2,1)S(1)}) custom-call(s32[3,32]{1,0:T(4,128)} %bitcast.3, s32[32]{0:T(128)} %cnt_in.1, s32[3,32]{1,0:T(4,128)} %bitcast.5, bf16[1,1,3,2,384,384]{5,4,3,2,1,0:T(8,128)(2,1)} %sigma.3, bf16[1,1,2,384,384]{4,3,2,1,0:T(8,128)(2,1)S(1)} %collective-permute-done.one, ...), custom_call_target="tpu_custom_call" | custom-call | flops 3000000000 | bytes 3538944 | tf_op jit(solution)/shard_map/centre/pallas_call | solution.py:260
  14.2 1.7 %collective-permute-start.6 = (bf16[256,768]{1,0:T(8,128)(2,1)S(1)}, bf16[256,768]{1,0:T(8,128)(2,1)S(1)}, u32[]{:S(2)}, u32[]{:S(2)}) collective-permute-start(bf16[256,768]{1,0:T(8,128)(2,1)S(1)} %get-tuple-element.22.early), channel_id=1, source_target_pairs={{0,8},{8,0},{16,24},{24,16},{32,40},{40,32},{48,56},{56,48},{64,72... | collective-permute-start | bytes 1179656 | tf_op jit(solution)/shard_map/ppermute | solution.py:220
  15.9 3.6 %collective-permute-start.7 = (bf16[256,768]{1,0:T(8,128)(2,1)S(1)}, bf16[256,768]{1,0:T(8,128)(2,1)S(1)}, u32[]{:S(2)}, u32[]{:S(2)}) collective-permute-start(bf16[256,768]{1,0:T(8,128)(2,1)S(1)} %get-tuple-element.22.early), channel_id=1, source_target_pairs={{8,16},{16,8},{24,32},{32,24},{40,48},{48,40},{56,64},{64,56},{72,... | collective-permute-start | bytes 1179656 | tf_op jit(solution)/shard_map/ppermute | solution.py:220
  19.5 2.1 %green.2 = (bf16[2304,768]{1,0:T(8,128)(2,1)S(1)}, bf16[384,768]{1,0:T(8,128)(2,1)S(1)}, bf16[384,1024]{1,0:T(8,128)(2,1)S(1)}, bf16[384,512]{1,0:T(8,128)(2,1)S(1)}) custom-call(bf16[1,1,3,2,384,384]{5,4,3,2,1,0:T(8,128)(2,1)} %green.3), custom_call_target="tpu_custom_call" | custom-call | flops 4000000000 | bytes 7077888 | tf_op jit(solution)/shard_map/green/pallas_call | solution.py:278
  21.7 1.2 %collective-permute-start.2 = (bf16[128,768]{1,0:T(8,128)(2,1)S(1)}, bf16[128,768]{1,0:T(8,128)(2,1)S(1)}, u32[]{:S(2)}, u32[]{:S(2)}) collective-permute-start(bf16[128,768]{1,0:T(8,128)(2,1)S(1)} %get-tuple-element.15.late), channel_id=1, source_target_pairs={{0,8},{8,0},{16,24},{24,16},{32,40},{40,32},{48,56},{56,48},{64,72... | collective-permute-start | bytes 589832 | tf_op jit(solution)/shard_map/ppermute | solution.py:220
  22.9 2.8 %local.1.partial = f32[384,768]{1,0:T(8,128)S(1)} custom-call(bf16[384,1536]{1,0:T(8,128)(2,1)S(1)} %get-tuple-element.16.first, bf16[256,768]{1,0:T(8,128)(2,1)S(1)} %get-tuple-element.22.early, bf16[128,768]{1,0:T(8,128)(2,1)S(1)} %get-tuple-element.15.late, bf16[384,1536]{1,0:T(8,128)(2,1)S(1)} %get-tuple-element.17.second, ...), custom_call_target="tpu_custom_call" | custom-call | flops 1811939328 | bytes 9437184 | tf_op jit(solution)/shard_map/local/pallas_call | solution.py:293
  25.7 7.9 %collective-permute-done.4.from_first = bf16[384,1536]{1,0:T(8,128)(2,1)S(1)} collective-permute-done((bf16[384,1536]{1,0:T(8,128)(2,1)S(1)}, bf16[384,1536]{1,0:T(8,128)(2,1)S(1)}, u32[]{:S(2)}, u32[]{:S(2)}) %collective-permute-start.4) | collective-permute-done | bytes 1179680 | tf_op jit(solution)/shard_map/ppermute | solution.py:220
  33.7 4.3 %collective-permute-start.3 = (bf16[128,768]{1,0:T(8,128)(2,1)S(1)}, bf16[128,768]{1,0:T(8,128)(2,1)S(1)}, u32[]{:S(2)}, u32[]{:S(2)}) collective-permute-start(bf16[128,768]{1,0:T(8,128)(2,1)S(1)} %get-tuple-element.15.late), channel_id=1, source_target_pairs={{8,16},{16,8},{24,32},{32,24},{40,48},{48,40},{56,64},{64,56},{72,... | collective-permute-start | bytes 589832 | tf_op jit(solution)/shard_map/ppermute | solution.py:220
  37.9 2.0 %collective-permute-done.5.from_second = bf16[384,1536]{1,0:T(8,128)(2,1)S(1)} collective-permute-done((bf16[384,1536]{1,0:T(8,128)(2,1)S(1)}, bf16[384,1536]{1,0:T(8,128)(2,1)S(1)}, u32[]{:S(2)}, u32[]{:S(2)}) %collective-permute-start.5) | collective-permute-done | bytes 1179680 | tf_op jit(solution)/shard_map/ppermute | solution.py:220
  40.0 2.0 %arrive.1 = (f32[384,768]{1,0:T(8,128)S(1)}, f32[384,768]{1,0:T(8,128)S(1)}) custom-call(bf16[384,1536]{1,0:T(8,128)(2,1)S(1)} %collective-permute-done.4.from_first, bf16[384,1536]{1,0:T(8,128)(2,1)S(1)} %collective-permute-done.5.from_second, bf16[2304,768]{1,0:T(8,128)(2,1)S(1)} %get-tuple-element.18.right), custom_call_target="tpu_custom_call" | custom-call | flops 1811939328 | bytes 9437184 | tf_op jit(solution)/shard_map/arrive/pallas_call | solution.py:302
  41.9 0.1 collective-permute-done.6.c_first
  42.1 6.3 %collective-permute-done.7.c_second = bf16[256,768]{1,0:T(8,128)(2,1)S(1)} collective-permute-done((bf16[256,768]{1,0:T(8,128)(2,1)S(1)}, bf16[256,768]{1,0:T(8,128)(2,1)S(1)}, u32[]{:S(2)}, u32[]{:S(2)}) %collective-permute-start.7) | collective-permute-done | bytes 393248 | tf_op jit(solution)/shard_map/ppermute | solution.py:220
  48.4 1.4 %early.1.partial = f32[384,768]{1,0:T(8,128)S(1)} custom-call(bf16[256,768]{1,0:T(8,128)(2,1)S(1)} %collective-permute-done.6.c_first, bf16[256,768]{1,0:T(8,128)(2,1)S(1)} %collective-permute-done.7.c_second, f32[384,768]{1,0:T(8,128)S(1)} %get-tuple-element.19.x_first, f32[384,768]{1,0:T(8,128)S(1)} %get-tuple-element.20.x_second, ...), custom_call_target="tpu_custom_call" | custom-call | flops 1358954496 | bytes 9437184 | tf_op jit(solution)/shard_map/early/pallas_call | solution.py:310
  49.8 0.0 collective-permute-done.2.c_first
  49.8 2.5 %collective-permute-done.3.c_second = bf16[128,768]{1,0:T(8,128)(2,1)S(1)} collective-permute-done((bf16[128,768]{1,0:T(8,128)(2,1)S(1)}, bf16[128,768]{1,0:T(8,128)(2,1)S(1)}, u32[]{:S(2)}, u32[]{:S(2)}) %collective-permute-start.3) | collective-permute-done | bytes 196640 | tf_op jit(solution)/shard_map/ppermute | solution.py:220
  52.3 1.8 %late.1 = f32[1,1,2,384,384]{4,3,2,1,0:T(8,128)} custom-call(bf16[128,768]{1,0:T(8,128)(2,1)S(1)} %collective-permute-done.2.c_first, bf16[128,768]{1,0:T(8,128)(2,1)S(1)} %collective-permute-done.3.c_second, f32[384,768]{1,0:T(8,128)S(1)} %get-tuple-element.19.x_first, f32[384,768]{1,0:T(8,128)S(1)} %get-tuple-element.20.x_second, ...), custom_call_target="tpu_custom_call" | custom-call | flops 905969664 | bytes 9437184 | tf_op jit(solution)/shard_map/late/pallas_call | solution.py:319
Async XLA Ops:
  0.0 9.5 %collective-permute-start = (bf16[1,1,2,384,384]{4,3,2,1,0:T(8,128)(2,1)}, bf16[1,1,2,384,384]{4,3,2,1,0:T(8,128)(2,1)S(1)}, u32[]{:S(2)}, u32[]{:S(2)}) collective-permute-start(bf16[1,1,2,384,384]{4,3,2,1,0:T(8,128)(2,1)} %param.8), channel_id=1, source_target_pairs={{0,1},{1,0},{2,3},{3,2},{4,5},{5,4},{6,7},{7,6},{8,9},{9,8},{10,11... | collective-permute-start | bytes 1769480 | tf_op jit(solution)/shard_map/ppermute | solution.py:220
  0.0 11.4 %collective-permute-start.1 = (bf16[1,1,2,384,384]{4,3,2,1,0:T(8,128)(2,1)}, bf16[1,1,2,384,384]{4,3,2,1,0:T(8,128)(2,1)S(1)}, u32[]{:S(2)}, u32[]{:S(2)}) collective-permute-start(bf16[1,1,2,384,384]{4,3,2,1,0:T(8,128)(2,1)} %param.8), channel_id=1, source_target_pairs={{1,2},{2,1},{3,4},{4,3},{5,6},{6,5},{9,10},{10,9},{11,12},{12,11},... | collective-permute-start | bytes 1769480 | tf_op jit(solution)/shard_map/ppermute | solution.py:220
  4.7 28.9 %collective-permute-start.4 = (bf16[384,1536]{1,0:T(8,128)(2,1)S(1)}, bf16[384,1536]{1,0:T(8,128)(2,1)S(1)}, u32[]{:S(2)}, u32[]{:S(2)}) collective-permute-start(bf16[384,1536]{1,0:T(8,128)(2,1)S(1)} %get-tuple-element.16.first), channel_id=1, source_target_pairs={{0,8},{8,0},{16,24},{24,16},{32,40},{40,32},{48,56},{56,48},{64,72... | collective-permute-start | bytes 3538952 | tf_op jit(solution)/shard_map/ppermute | solution.py:220
  5.9 34.0 %collective-permute-start.5 = (bf16[384,1536]{1,0:T(8,128)(2,1)S(1)}, bf16[384,1536]{1,0:T(8,128)(2,1)S(1)}, u32[]{:S(2)}, u32[]{:S(2)}) collective-permute-start(bf16[384,1536]{1,0:T(8,128)(2,1)S(1)} %get-tuple-element.17.second), channel_id=1, source_target_pairs={{8,16},{16,8},{24,32},{32,24},{40,48},{48,40},{56,64},{64,56},{72,... | collective-permute-start | bytes 3538952 | tf_op jit(solution)/shard_map/ppermute | solution.py:220
  14.2 27.8 %collective-permute-start.6 = (bf16[256,768]{1,0:T(8,128)(2,1)S(1)}, bf16[256,768]{1,0:T(8,128)(2,1)S(1)}, u32[]{:S(2)}, u32[]{:S(2)}) collective-permute-start(bf16[256,768]{1,0:T(8,128)(2,1)S(1)} %get-tuple-element.22.early), channel_id=1, source_target_pairs={{0,8},{8,0},{16,24},{24,16},{32,40},{40,32},{48,56},{56,48},{64,72... | collective-permute-start | bytes 1179656 | tf_op jit(solution)/shard_map/ppermute | solution.py:220
  15.9 32.5 %collective-permute-start.7 = (bf16[256,768]{1,0:T(8,128)(2,1)S(1)}, bf16[256,768]{1,0:T(8,128)(2,1)S(1)}, u32[]{:S(2)}, u32[]{:S(2)}) collective-permute-start(bf16[256,768]{1,0:T(8,128)(2,1)S(1)} %get-tuple-element.22.early), channel_id=1, source_target_pairs={{8,16},{16,8},{24,32},{32,24},{40,48},{48,40},{56,64},{64,56},{72,... | collective-permute-start | bytes 1179656 | tf_op jit(solution)/shard_map/ppermute | solution.py:220
  21.7 28.1 %collective-permute-start.2 = (bf16[128,768]{1,0:T(8,128)(2,1)S(1)}, bf16[128,768]{1,0:T(8,128)(2,1)S(1)}, u32[]{:S(2)}, u32[]{:S(2)}) collective-permute-start(bf16[128,768]{1,0:T(8,128)(2,1)S(1)} %get-tuple-element.15.late), channel_id=1, source_target_pairs={{0,8},{8,0},{16,24},{24,16},{32,40},{40,32},{48,56},{56,48},{64,72... | collective-permute-start | bytes 589832 | tf_op jit(solution)/shard_map/ppermute | solution.py:220
  33.7 18.7 %collective-permute-start.3 = (bf16[128,768]{1,0:T(8,128)(2,1)S(1)}, bf16[128,768]{1,0:T(8,128)(2,1)S(1)}, u32[]{:S(2)}, u32[]{:S(2)}) collective-permute-start(bf16[128,768]{1,0:T(8,128)(2,1)S(1)} %get-tuple-element.15.late), channel_id=1, source_target_pairs={{8,16},{16,8},{24,32},{32,24},{40,48},{48,40},{56,64},{64,56},{72,... | collective-permute-start | bytes 589832 | tf_op jit(solution)/shard_map/ppermute | solution.py:220

commit v4 on v3

--- a/solution.py
+++ b/solution.py
@@ -1,3 +1,5 @@
+import functools
+
 import jax
 import jax.numpy as jnp
 from jax import lax
@@ -10,6 +12,8 @@
 BF16 = jnp.bfloat16
 VMEM_LIMIT = 24 * 1024 * 1024
 CHUNKS = 3
+PIECE = 48
+LEVELS = (192, 288, 384)
 SPLIT = 256
 
 
@@ -43,13 +47,57 @@
     return rows, cols
 
 
-def side_kernel(off_in, cnt_in, rng_in, sigma, first, second, off, cnt, rng, held, sems, table_sems):
+def packing(reach, width):
+    if reach == width:
+        return 2 * width, width, 0
+    body = reach // 128 * 128
+    groups = 2 * body // 128 + 1
+    lanes = 2 * width // 128
+    return width + groups * (reach // PIECE) // lanes * PIECE, body, reach - body
+
+
+def unit_at(group, piece, reach, width):
+    lanes = 2 * width // 128
+    unit = group * (reach // PIECE) + piece
+    return width + unit // lanes * PIECE, unit % lanes * 128
+
+
+def widest_small(off, cnt, rng):
+    slots = lax.broadcasted_iota(jnp.int32, off.shape, 0)
+    live = slots < cnt[...]
+
+    def reach(offset):
+        return jnp.max(jnp.where(live & (off[...] == offset), rng[...], 0), axis=0, keepdims=True)
+
+    low = jnp.minimum(reach(-1), reach(-2))
+    high = jnp.minimum(reach(1), reach(2))
+    return jnp.max(jnp.maximum(low, high))
+
+
+def near_leads(slab, d, off, cnt, rng):
+    near, far = [
+        functools.reduce(jnp.maximum, [reach for _, reach in matches(slab, offset, off, cnt, rng)])
+        for offset in (d, 2 * d)
+    ]
+    return near >= far
+
+
+def side_kernel(off_in, cnt_in, rng_in, sigma, *refs):
+    outs, (level, roles) = refs[: 2 * len(LEVELS)], refs[2 * len(LEVELS) : 2 * len(LEVELS) + 2]
+    off, cnt, rng, off_v, cnt_v, rng_v, held, sems, table_sems = refs[2 * len(LEVELS) + 2 :]
     slab = lax.axis_index("slab")
     s = toward()
     chunks, slots, _, height, width = held.shape
+    moves = (
+        (off_in, off_v),
+        (cnt_in, cnt_v),
+        (rng_in, rng_v),
+        (off_in, off),
+        (cnt_in, cnt),
+        (rng_in, rng),
+    )
     tables = [
-        pltpu.make_async_copy(src, dst, table_sems.at[n])
-        for n, (src, dst) in enumerate(((off_in, off), (cnt_in, cnt), (rng_in, rng)))
+        pltpu.make_async_copy(src, dst, table_sems.at[n]) for n, (src, dst) in enumerate(moves)
     ]
     copies = [
         pltpu.make_async_copy(
@@ -61,44 +109,90 @@
         copy.start()
     for copy in tables:
         copy.wait()
-    wanted = (
-        (first, 0, s),
-        (first, 1, 2 * s),
-        (second, 0, -2 * s),
-        (second, 1, -s),
-    )
+    widest = widest_small(off_v, cnt_v, rng_v)
+    rank = sum((widest > reach).astype(jnp.int32) for reach in LEVELS[:-1])
+    level[0] = rank
+    cnt = cnt.at[0]
+    last = off.shape[1] - 1
+    for n, d in enumerate((s, -s)):
+        neighbour = jnp.clip(slab + d, 0, last)
+        roles[n] = near_leads(neighbour, -d, off, cnt, rng).astype(jnp.int32)
+
+    merges, messages = [], []
+    for d in (s, -s):
+        sides = []
+        for offset in (d, 2 * d):
+            found = matches(slab, offset, off, cnt, rng)
+            number = sum(live for live, _ in found)
+            which = jnp.int32(0)
+            for q in reversed(range(slots)):
+                which = jnp.where(found[q][0] > 0, q, which)
+            reach = functools.reduce(jnp.maximum, [reach for _, reach in found])
+            merges.append((number, which, [reach for _, reach in found]))
+            sides.append((which, reach))
+        near, far = sides
+        leads = near[1] >= far[1]
+        big = tuple(jnp.where(leads, u, v) for u, v in zip(near, far))
+        small = tuple(jnp.where(leads, v, u) for u, v in zip(near, far))
+        messages.append((big, small))
+
     for c in range(chunks):
         copies[c].wait()
         rows, cols = index_grid(c * height, height, width)
-        top = pl.ds(c * height, height)
-        for out, slot, offset in wanted:
-            found = matches(slab, offset, off, cnt, rng)
-            number = sum(live for live, _ in found)
-            which = sum(q * live for q, (live, _) in enumerate(found))
-            limit = sum(reach for _, reach in found)
-            at = [pl.ds((2 * slot + part) * width, width) for part in range(2)]
-
-            @pl.when(number == 0)
-            def _():
-                for part in range(2):
-                    out[top, at[part]] = jnp.zeros((height, width), BF16)
-
-            @pl.when(number == 1)
-            def _():
-                for part in range(2):
-                    out[top, at[part]] = masked(held[c, which, part], rows, cols, limit).astype(BF16)
+        for number, which, reaches in merges:
 
             @pl.when(number > 1)
             def _():
                 for part in range(2):
                     total = jnp.zeros((height, width), F32)
                     for q in range(slots):
-                        total = total + masked(held[c, q, part], rows, cols, found[q][1])
-                    out[top, at[part]] = total.astype(BF16)
-
-
-def centre_kernel(off, cnt, rng, sigma, one, two, early, late):
+                        total = total + masked(held[c, q, part], rows, cols, reaches[q])
+                    held[c, which, part] = total.astype(BF16)
+
+        for n, (big, small) in enumerate(messages):
+            for index, reach in enumerate(LEVELS):
+                out = outs[2 * index + n]
+
+                @pl.when(rank == index)
+                def _():
+                    for part in range(2):
+                        block = masked(held[c, big[0], part], rows, cols, big[1])
+                        out[c * height : (c + 1) * height, part * width : (part + 1) * width] = (
+                            block.astype(BF16)
+                        )
+                    _, body, rest = packing(reach, width)
+                    if rest == 0:
+                        for part in range(2):
+                            block = masked(held[c, small[0], part], rows, cols, small[1])
+                            first = width + c * height
+                            out[first : first + height, part * width : (part + 1) * width] = (
+                                block.astype(BF16)
+                            )
+                        return
+                    for piece in range(c * height // PIECE, (c + 1) * height // PIECE):
+                        if piece >= reach // PIECE:
+                            continue
+                        first = piece * PIECE - c * height
+                        inner = slice(first, first + PIECE)
+                        parts = [
+                            masked(
+                                held[c, small[0], part, inner, : body + 128],
+                                rows[inner, : body + 128],
+                                cols[inner, : body + 128],
+                                small[1],
+                            )
+                            for part in range(2)
+                        ]
+                        units = [part[:, at : at + 128] for part in parts for at in range(0, body, 128)]
+                        units.append(parts[0][:, body:] + pltpu.roll(parts[1][:, body:], rest, 1))
+                        for group, unit in enumerate(units):
+                            row, lane = unit_at(group, piece, reach, width)
+                            out[row : row + PIECE, lane : lane + 128] = unit.astype(BF16)
+
+
+def centre_kernel(off, cnt, rng, sigma, one, two, early, late, near_first, near_second):
     slab = lax.axis_index("slab")
+    cnt = cnt.at[0]
     step = pl.program_id(0)
     height, width = sigma.shape[-2:]
     rows, cols = index_grid(step * height, height, width)
@@ -109,6 +203,11 @@
         for q in range(sigma.shape[2]):
             total = total + masked(sigma[0, 0, q, part], rows, cols, found[q][1])
         at = pl.ds(part * width, width)
+        for d, out in ((toward(), near_first), (-toward(), near_second)):
+            near = jnp.zeros((height, width), F32)
+            for q, (_, reach) in enumerate(matches(slab, d, off, cnt, rng)):
+                near = near + masked(sigma[0, 0, q, part], rows, cols, reach)
+            out[:, at] = near.astype(BF16)
 
         @pl.when(step < SPLIT // height)
         def _():
@@ -152,19 +251,45 @@
     out[first + height : first + 2 * height, width:] = real
 
 
-def local_kernel(first, early, late, second, right, left, out, held):
+def local_kernel(near_first, early, late, near_second, right, left, out, held):
     wide = early.shape[1]
-    x = dot(first[:, :wide], right[:wide]) + dot(second[:, wide:], right[2 * wide :])
+    x = dot(near_first[...], right[:wide]) + dot(near_second[...], right[2 * wide :])
     middle = right[wide : 2 * wide]
     x = x + jnp.concatenate([dot(early[...], middle), dot(late[...], middle)], axis=0)
     spread(x, held, 0)
     out[...] = dot(left[...], held[...])
 
 
-def arrive_kernel(from_first, from_second, right, out_first, out_second):
-    wide = out_first.shape[1]
-    out_first[...] = dot(from_first[...], right[wide:])
-    out_second[...] = dot(from_second[...], right[: 2 * wide])
+def arrive_kernel(reach, roles, from_first, from_second, right, out_first, out_second, *packed):
+    width, wide = out_first.shape
+    for n, (message, out, other) in enumerate(
+        ((from_first, out_first, 2 * wide), (from_second, out_second, 0))
+    ):
+        leads = roles[n] > 0
+        big_at = pl.multiple_of(jnp.where(leads, wide, other), wide)
+        small_at = pl.multiple_of(jnp.where(leads, other, wide), wide)
+        total = dot(message[:width], right[pl.ds(big_at, wide)])
+        if reach == width:
+            out[...] = total + dot(message[width:], right[pl.ds(small_at, wide)])
+            continue
+        left, down = packed
+        _, body, rest = packing(reach, width)
+        for group in range(2 * body // 128 + 1):
+            for piece in range(reach // PIECE):
+                row, lane = unit_at(group, piece, reach, width)
+                left[piece * PIECE : (piece + 1) * PIECE, group * 128 : (group + 1) * 128] = (
+                    message[row : row + PIECE, lane : lane + 128]
+                )
+        for part in range(2):
+            source = pl.multiple_of(small_at + part * width, width)
+            down[part * body : (part + 1) * body] = right[pl.ds(source, body)]
+            tail = pl.multiple_of(small_at + part * width + body, 128)
+            to = 2 * body + part * rest
+            down[to : to + rest] = right[pl.ds(tail, rest)]
+        if 2 * rest < 128:
+            down[2 * body + 2 * rest :] = jnp.zeros((128 - 2 * rest, wide), BF16)
+        out[:reach] = total[:reach] + dot(left[...], down[...])
+        out[reach:] = total[reach:]
 
 
 def fold(c_first, c_second, x_first, x_second, right, held, first):
@@ -228,26 +353,45 @@
     width = green.shape[-1]
     wide = 2 * width
     slots = sigma.shape[2]
-    tables = (pair_off.T, pair_count, pair_range.T)
+    tables = (pair_off.T, pair_count[None], pair_range.T)
     block_bytes = 2 * width * wide
-    height = width // CHUNKS
-
-    first, second = pl.pallas_call(
+    chunks = width // (2 * PIECE)
+
+    messages = []
+    for reach in LEVELS:
+        rows = packing(reach, width)[0]
+        messages += [jax.ShapeDtypeStruct((rows, wide), BF16)] * 2
+    *messages, level, roles = pl.pallas_call(
         side_kernel,
         in_specs=[hbm()] * 4,
-        out_shape=[jax.ShapeDtypeStruct((width, 2 * wide), BF16)] * 2,
+        out_specs=[pl.BlockSpec(memory_space=pltpu.VMEM)] * len(messages) + [smem(), smem()],
+        out_shape=[
+            *messages,
+            jax.ShapeDtypeStruct((1,), jnp.int32),
+            jax.ShapeDtypeStruct((2,), jnp.int32),
+        ],
         scratch_shapes=[
-            pltpu.SMEM(tables[0].shape, jnp.int32),
-            pltpu.SMEM(tables[1].shape, jnp.int32),
-            pltpu.SMEM(tables[2].shape, jnp.int32),
-            pltpu.VMEM((CHUNKS, slots, 2, height, width), BF16),
-            pltpu.SemaphoreType.DMA((CHUNKS,)),
-            pltpu.SemaphoreType.DMA((3,)),
+            *[pltpu.SMEM(table.shape, jnp.int32) for table in tables],
+            *[pltpu.VMEM(table.shape, jnp.int32) for table in tables],
+            pltpu.VMEM((chunks, slots, 2, 2 * PIECE, width), BF16),
+            pltpu.SemaphoreType.DMA((chunks,)),
+            pltpu.SemaphoreType.DMA((6,)),
         ],
         compiler_params=params(),
         cost_estimate=cost(3e9, 7 * block_bytes),
         name="side",
     )(*[in_hbm(value) for value in (*tables, sigma)])
+    branches = [functools.partial(remainder, reach, 2 * n) for n, reach in enumerate(LEVELS)]
+    return lax.switch(level[0], branches, messages, roles, green, sigma, phonon, tables)
+
+
+def remainder(reach, index, messages, roles, green, sigma, phonon, tables):
+    first, second = messages[index : index + 2]
+    width = green.shape[-1]
+    wide = 2 * width
+    slots = sigma.shape[2]
+    block_bytes = 2 * width * wide
+    height = width // CHUNKS
     from_first = swap(first, "slab", 0)
     from_second = swap(second, "slab", 1)
 
@@ -257,14 +401,17 @@
     sigma_spec = pl.BlockSpec((1, 1, slots, 2, height, width), lambda c: (0, 0, 0, 0, c, 0))
     phonon_spec = pl.BlockSpec((1, 1, 2, height, width), lambda c: (0, 0, 0, c, 0))
     whole = lambda rows: pl.BlockSpec((rows, wide), lambda c: (0, 0))
-    early, late = pl.pallas_call(
+    chunk = pl.BlockSpec((height, wide), lambda c: (c, 0))
+    early, late, near_first, near_second = pl.pallas_call(
         centre_kernel,
         grid=(CHUNKS,),
         in_specs=[smem(), smem(), smem(), sigma_spec, phonon_spec, phonon_spec],
-        out_specs=[whole(SPLIT), whole(width - SPLIT)],
+        out_specs=[whole(SPLIT), whole(width - SPLIT), chunk, chunk],
         out_shape=[
             jax.ShapeDtypeStruct((SPLIT, wide), BF16),
             jax.ShapeDtypeStruct((width - SPLIT, wide), BF16),
+            jax.ShapeDtypeStruct((width, wide), BF16),
+            jax.ShapeDtypeStruct((width, wide), BF16),
         ],
         compiler_params=params(),
         cost_estimate=cost(3e9, 6 * block_bytes),
@@ -297,15 +444,20 @@
         compiler_params=params(),
         cost_estimate=cost(4 * unit, 16 * block_bytes),
         name="local",
-    )(first, early, late, second, right, left)
-
+    )(near_first, early, late, near_second, right, left)
+
+    _, body, rest = packing(reach, width)
+    depth = 2 * body + 128
+    packed = [pltpu.VMEM((reach, depth), BF16), pltpu.VMEM((depth, wide), BF16)]
     x_first, x_second = pl.pallas_call(
-        arrive_kernel,
+        functools.partial(arrive_kernel, reach),
+        in_specs=[smem()] + [pl.BlockSpec(memory_space=pltpu.VMEM)] * 3,
         out_shape=[square, square],
+        scratch_shapes=packed if rest else [],
         compiler_params=params(),
         cost_estimate=cost(4 * unit, 16 * block_bytes),
         name="arrive",
-    )(from_first, from_second, right)
+    )(roles, from_first, from_second, right)
 
     partial = pl.pallas_call(
         early_kernel,
@@ -319,7 +471,7 @@
     return pl.pallas_call(
         late_kernel,
         out_specs=hbm(),
-        out_shape=jax.ShapeDtypeStruct((1, 1, 2, width, width), F32),
+        out_shape=pltpu.HBM((1, 1, 2, width, width), F32),
         scratch_shapes=[
             pltpu.VMEM((4 * (width - SPLIT), wide), BF16),
             pltpu.VMEM((2, width, width), F32),

time: 54.5 us -> 52.1 us (0.956)
  waiting for transfers between devices: 20.8 us -> 16.4 us
  Pallas kernels: 15.1 us -> 17.3 us
  starting transfers between devices: 18.1 us -> 16.5 us
  loops' own time: 0 us -> 0.65 us
  between operations: 0.26 us -> 0.89 us
    ppermute x8, waiting for transfers between devices: 20.8 us -> 16.4 us  [swap(): return lax.ppermute(value, axis, swaps(first, lax.axis_size(axis)))]
    pallas_call x7, Pallas kernels: 15.1 us -> 17.3 us  [the longest x1 3.43 us: remainder(): pl.pallas_call(centre_kernel, grid=(CHUNKS,), in_specs=[smem(), smem(), s...]
    ppermute x8, starting transfers between devices: 18.1 us -> 16.5 us  [swap(): return lax.ppermute(value, axis, swaps(first, lax.axis_size(axis)))]
    another operation x0 -> x1, loops' own time: none -> 0.65 us  [program(): lax.switch(level[0], branches, messages, roles, green, sigma, phonon, tab...]
  transfers between devices with their start and end apart: 8 -> 8, of which waited for: 6 -> 5; matrix products, arithmetic and copies ran while one was open for 0% -> 0% of each run, Pallas kernels for 25% -> 24%
where the time goes in v4:
time: 52.1 us; the launch traced here: 51.8 us
  Pallas kernels  17.3 us (33%)
  starting transfers between devices  16.5 us (32%)
  waiting for transfers between devices  16.4 us (31%)
  between operations  0.89 us (2%)
  loops' own time  0.65 us (1%)
    ppermute x8, starting transfers between devices, swap(): return lax.ppermute(value, axis, swaps(first, lax.axis_size(axis)))  16.5 us
    ppermute x8, waiting for transfers between devices, swap(): return lax.ppermute(value, axis, swaps(first, lax.axis_size(axis)))  16.4 us
    pallas_call x1, Pallas kernels, remainder(): pl.pallas_call(centre_kernel, grid=(CHUNKS,), in_specs=[smem(), smem(), s...  3.43 us
    pallas_call x1, Pallas kernels, program(): pl.pallas_call(side_kernel, in_specs=[hbm()] * 4, out_specs=[pl.BlockSpec...  3.33 us
    pallas_call x1, Pallas kernels, remainder(): pl.pallas_call(local_kernel, out_shape=square, scratch_shapes=[pltpu.VMEM...  2.84 us
    pallas_call x1, Pallas kernels, remainder(): pl.pallas_call(functools.partial(arrive_kernel, reach), in_specs=[smem()]...  2.38 us
    pallas_call x1, Pallas kernels, remainder(): pl.pallas_call(green_kernel, out_shape=[jax.ShapeDtypeStruct((3 * wide, w...  2.12 us
    pallas_call x1, Pallas kernels, remainder(): pl.pallas_call(late_kernel, out_specs=hbm(), out_shape=pltpu.HBM((1, 1, 2...  1.78 us
  transfers between devices with their start and end apart: 8, of which 5 were waited for; matrix products, arithmetic and copies ran while one was open for 0% of the time, Pallas kernels for 24%

profile of v4, /device:TPU:130, one launch (start us, length us, event | category | flops | bytes accessed | tf_op | source)
XLA Modules:
  0.0 51.8 jit_solution(12280785039991974456)
XLA Ops:
  0.0 0.0 copy-start
  0.0 3.3 %side.1 = (bf16[480,768]{1,0:T(8,128)(2,1)S(1)}, bf16[480,768]{1,0:T(8,128)(2,1)S(1)}, bf16[624,768]{1,0:T(8,128)(2,1)S(1)}, bf16[624,768]{1,0:T(8,128)(2,1)S(1)...) custom-call(s32[3,32]{1,0:T(4,128)} %bitcast.4, s32[1,32]{1,0:T(1,128)} %bitcast.12, ...), custom_call_target="tpu_custom_call" | custom-call | flops 3000000000 | bytes 4128768 | tf_op jit(solution)/shard_map/side/pallas_call | solution.py:364
  4.0 0.0 copy-done
  4.0 47.5 %conditional.1 = (f32[1,1,2,384,384]{4,3,2,1,0:T(8,128)}) conditional(s32[]{:T(128)} %bitcast.3, (bf16[1,1,2,384,384]{4,3,2,1,0:T(8,128)(2,1)S(1)}, s32[3,32]{1,0:T(4,128)}, s32[1,32]{1,0:T(1,128)}, s32[3,32]{1,0:T(4,128)}, bf16[1,1,3,2,384,384]{5,4,3,2,1,0:T(8,128)(2,1)}, /*index=5*/bf16[480,768]{1,0:T(8,128)(2,1)S(1)}, ...), branch_computations={%region_0.0_spmd, %region_1.0_spmd, %region_2.0_spmd} | conditional | flops 12888803328 | bytes 67240264 | solution.py:385
  4.2 0.1 collective-permute-start.8
  4.3 2.5 %collective-permute-start.9 = (bf16[1,1,2,384,384]{4,3,2,1,0:T(8,128)(2,1)S(1)}, bf16[1,1,2,384,384]{4,3,2,1,0:T(8,128)(2,1)S(1)}, u32[]{:S(2)}, u32[]{:S(2)}) collective-permute-start(bf16[1,1,2,384,384]{4,3,2,1,0:T(8,128)(2,1)S(1)} %get-tuple-element.86), channel_id=1, source_target_pairs={{1,2},{2,1},{3,4},{4,3},{5,6},{6,5},{9,10},{10,9},{11,12},{12,11},... | collective-permute-start | bytes 1769480 | tf_op jit(solution)/shard_map/cond/branch_1_fun/ppermute | solution.py:345
  6.9 0.9 %collective-permute-start.12 = (bf16[624,768]{1,0:T(8,128)(2,1)S(1)}, bf16[624,768]{1,0:T(8,128)(2,1)S(1)}, u32[]{:S(2)}, u32[]{:S(2)}) collective-permute-start(bf16[624,768]{1,0:T(8,128)(2,1)S(1)} %get-tuple-element.89), channel_id=1, source_target_pairs={{0,8},{8,0},{16,24},{24,16},{32,40},{40,32},{48,56},{56,48},{64,72... | collective-permute-start | bytes 2875400 | tf_op jit(solution)/shard_map/cond/branch_1_fun/ppermute | solution.py:345
  7.8 3.6 %collective-permute-start.13 = (bf16[624,768]{1,0:T(8,128)(2,1)S(1)}, bf16[624,768]{1,0:T(8,128)(2,1)S(1)}, u32[]{:S(2)}, u32[]{:S(2)}) collective-permute-start(bf16[624,768]{1,0:T(8,128)(2,1)S(1)} %get-tuple-element.90), channel_id=1, source_target_pairs={{8,16},{16,8},{24,32},{32,24},{40,48},{48,40},{56,64},{64,56},{72,... | collective-permute-start | bytes 2875400 | tf_op jit(solution)/shard_map/cond/branch_1_fun/ppermute | solution.py:345
  11.4 0.0 collective-permute-done.8.one
  11.4 4.1 %collective-permute-done.9.two = bf16[1,1,2,384,384]{4,3,2,1,0:T(8,128)(2,1)S(1)} collective-permute-done((bf16[1,1,2,384,384]{4,3,2,1,0:T(8,128)(2,1)S(1)}, bf16[1,1,2,384,384]{4,3,2,1,0:T(8,128)(2,1)S(1)}, u32[]{:S(2)}, u32[]{:S(2)}) %collective-permute-start.9) | collective-permute-done | bytes 589856 | tf_op jit(solution)/shard_map/cond/branch_1_fun/ppermute | solution.py:345
  15.5 3.4 %centre.4 = (bf16[256,768]{1,0:T(8,128)(2,1)S(1)}, bf16[128,768]{1,0:T(8,128)(2,1)S(1)}, bf16[384,768]{1,0:T(8,128)(2,1)S(1)}, bf16[384,768]{1,0:T(8,128)(2,1)S(1)}) custom-call(s32[3,32]{1,0:T(4,128)} %get-tuple-element.82.off, s32[1,32]{1,0:T(1,128)} %get-tuple-element.83.cnt, s32[3,32]{1,0:T(4,128)} %get-tuple-element.84.rng, ...), custom_call_target="tpu_custom_call" | custom-call | flops 3000000000 | bytes 3538944 | tf_op jit(solution)/shard_map/cond/branch_1_fun/centre/pallas_call | solution.py:405
  19.0 0.9 %collective-permute-start.14 = (bf16[256,768]{1,0:T(8,128)(2,1)S(1)}, bf16[256,768]{1,0:T(8,128)(2,1)S(1)}, u32[]{:S(2)}, u32[]{:S(2)}) collective-permute-start(bf16[256,768]{1,0:T(8,128)(2,1)S(1)} %get-tuple-element.96.early), channel_id=1, source_target_pairs={{0,8},{8,0},{16,24},{24,16},{32,40},{40,32},{48,56},{56,48},{64,72... | collective-permute-start | bytes 1179656 | tf_op jit(solution)/shard_map/cond/branch_1_fun/ppermute | solution.py:345
  19.9 3.6 %collective-permute-start.15 = (bf16[256,768]{1,0:T(8,128)(2,1)S(1)}, bf16[256,768]{1,0:T(8,128)(2,1)S(1)}, u32[]{:S(2)}, u32[]{:S(2)}) collective-permute-start(bf16[256,768]{1,0:T(8,128)(2,1)S(1)} %get-tuple-element.96.early), channel_id=1, source_target_pairs={{8,16},{16,8},{24,32},{32,24},{40,48},{48,40},{56,64},{64,56},{72,... | collective-permute-start | bytes 1179656 | tf_op jit(solution)/shard_map/cond/branch_1_fun/ppermute | solution.py:345
  23.5 2.1 %green.4 = (bf16[2304,768]{1,0:T(8,128)(2,1)S(1)}, bf16[384,768]{1,0:T(8,128)(2,1)S(1)}, bf16[384,1024]{1,0:T(8,128)(2,1)S(1)}, bf16[384,512]{1,0:T(8,128)(2,1)S(1)}) custom-call(bf16[1,1,3,2,384,384]{5,4,3,2,1,0:T(8,128)(2,1)} %get-tuple-element.91.green), custom_call_target="tpu_custom_call" | custom-call | flops 4000000000 | bytes 7077888 | tf_op jit(solution)/shard_map/cond/branch_1_fun/green/pallas_call | solution.py:425
  25.6 1.2 %collective-permute-start.10 = (bf16[128,768]{1,0:T(8,128)(2,1)S(1)}, bf16[128,768]{1,0:T(8,128)(2,1)S(1)}, u32[]{:S(2)}, u32[]{:S(2)}) collective-permute-start(bf16[128,768]{1,0:T(8,128)(2,1)S(1)} %get-tuple-element.87.late), channel_id=1, source_target_pairs={{0,8},{8,0},{16,24},{24,16},{32,40},{40,32},{48,56},{56,48},{64,72... | collective-permute-start | bytes 589832 | tf_op jit(solution)/shard_map/cond/branch_1_fun/ppermute | solution.py:345
  26.9 2.8 %local.4.partial = f32[384,768]{1,0:T(8,128)S(1)} custom-call(bf16[384,768]{1,0:T(8,128)(2,1)S(1)} %get-tuple-element.98.near_first, bf16[256,768]{1,0:T(8,128)(2,1)S(1)} %get-tuple-element.96.early, bf16[128,768]{1,0:T(8,128)(2,1)S(1)} %get-tuple-element.87.late, bf16[384,768]{1,0:T(8,128)(2,1)S(1)} %get-tuple-element.99.near_second, ...), custom_call_target="tpu_custom_call" | custom-call | flops 1811939328 | bytes 9437184 | tf_op jit(solution)/shard_map/cond/branch_1_fun/local/pallas_call | solution.py:440
  29.7 1.4 %collective-permute-done.12.from_first = bf16[624,768]{1,0:T(8,128)(2,1)S(1)} collective-permute-done((bf16[624,768]{1,0:T(8,128)(2,1)S(1)}, bf16[624,768]{1,0:T(8,128)(2,1)S(1)}, u32[]{:S(2)}, u32[]{:S(2)}) %collective-permute-start.12) | collective-permute-done | bytes 958496 | tf_op jit(solution)/shard_map/cond/branch_1_fun/ppermute | solution.py:345
  31.1 3.7 %collective-permute-start.11 = (bf16[128,768]{1,0:T(8,128)(2,1)S(1)}, bf16[128,768]{1,0:T(8,128)(2,1)S(1)}, u32[]{:S(2)}, u32[]{:S(2)}) collective-permute-start(bf16[128,768]{1,0:T(8,128)(2,1)S(1)} %get-tuple-element.87.late), channel_id=1, source_target_pairs={{8,16},{16,8},{24,32},{32,24},{40,48},{48,40},{56,64},{64,56},{72,... | collective-permute-start | bytes 589832 | tf_op jit(solution)/shard_map/cond/branch_1_fun/ppermute | solution.py:345
  34.7 2.3 %collective-permute-done.13.from_second = bf16[624,768]{1,0:T(8,128)(2,1)S(1)} collective-permute-done((bf16[624,768]{1,0:T(8,128)(2,1)S(1)}, bf16[624,768]{1,0:T(8,128)(2,1)S(1)}, u32[]{:S(2)}, u32[]{:S(2)}) %collective-permute-start.13) | collective-permute-done | bytes 958496 | tf_op jit(solution)/shard_map/cond/branch_1_fun/ppermute | solution.py:345
  37.1 2.4 %arrive.4 = (f32[384,768]{1,0:T(8,128)S(1)}, f32[384,768]{1,0:T(8,128)S(1)}) custom-call(s32[2]{0:T(128)S(1)} %get-tuple-element.88.roles, bf16[624,768]{1,0:T(8,128)(2,1)S(1)} %collective-permute-done.12.from_first, bf16[624,768]{1,0:T(8,128)(2,1)S(1)} %collective-permute-done.13.from_second, bf16[2304,768]{1,0:T(8,128)(2,1)S(1)} %get-tuple-element.92.right), custom_call_target="tpu_custom_call" | custom-call | flops 1811939328 | bytes 9437184 | tf_op jit(solution)/shard_map/cond/branch_1_fun/arrive/pallas_call | solution.py:452
  39.5 0.0 collective-permute-done.14.c_first
  39.5 6.0 %collective-permute-done.15.c_second = bf16[256,768]{1,0:T(8,128)(2,1)S(1)} collective-permute-done((bf16[256,768]{1,0:T(8,128)(2,1)S(1)}, bf16[256,768]{1,0:T(8,128)(2,1)S(1)}, u32[]{:S(2)}, u32[]{:S(2)}) %collective-permute-start.15) | collective-permute-done | bytes 393248 | tf_op jit(solution)/shard_map/cond/branch_1_fun/ppermute | solution.py:345
  45.5 1.4 %early.4.partial = f32[384,768]{1,0:T(8,128)S(1)} custom-call(bf16[256,768]{1,0:T(8,128)(2,1)S(1)} %collective-permute-done.14.c_first, bf16[256,768]{1,0:T(8,128)(2,1)S(1)} %collective-permute-done.15.c_second, f32[384,768]{1,0:T(8,128)S(1)} %get-tuple-element.93.x_first, f32[384,768]{1,0:T(8,128)S(1)} %get-tuple-element.94.x_second, ...), custom_call_target="tpu_custom_call" | custom-call | flops 1358954496 | bytes 9437184 | tf_op jit(solution)/shard_map/cond/branch_1_fun/early/pallas_call | solution.py:462
  46.9 0.0 collective-permute-done.10.c_first
  46.9 2.5 %collective-permute-done.11.c_second = bf16[128,768]{1,0:T(8,128)(2,1)S(1)} collective-permute-done((bf16[128,768]{1,0:T(8,128)(2,1)S(1)}, bf16[128,768]{1,0:T(8,128)(2,1)S(1)}, u32[]{:S(2)}, u32[]{:S(2)}) %collective-permute-start.11) | collective-permute-done | bytes 196640 | tf_op jit(solution)/shard_map/cond/branch_1_fun/ppermute | solution.py:345
  49.4 1.8 %late.4 = f32[1,1,2,384,384]{4,3,2,1,0:T(8,128)} custom-call(bf16[128,768]{1,0:T(8,128)(2,1)S(1)} %collective-permute-done.10.c_first, bf16[128,768]{1,0:T(8,128)(2,1)S(1)} %collective-permute-done.11.c_second, f32[384,768]{1,0:T(8,128)S(1)} %get-tuple-element.93.x_first, f32[384,768]{1,0:T(8,128)S(1)} %get-tuple-element.94.x_second, ...), custom_call_target="tpu_custom_call" | custom-call | flops 905969664 | bytes 9437184 | tf_op jit(solution)/shard_map/cond/branch_1_fun/late/pallas_call | solution.py:471
Async XLA Ops:
  0.0 4.0 %copy-start = (bf16[1,1,2,384,384]{4,3,2,1,0:T(8,128)(2,1)S(1)}, bf16[1,1,2,384,384]{4,3,2,1,0:T(8,128)(2,1)}, u32[]{:S(2)}) copy-start(bf16[1,1,2,384,384]{4,3,2,1,0:T(8,128)(2,1)} %param.11) | copy-start | bytes 1769476
  4.2 7.2 %collective-permute-start.8 = (bf16[1,1,2,384,384]{4,3,2,1,0:T(8,128)(2,1)S(1)}, bf16[1,1,2,384,384]{4,3,2,1,0:T(8,128)(2,1)S(1)}, u32[]{:S(2)}, u32[]{:S(2)}) collective-permute-start(bf16[1,1,2,384,384]{4,3,2,1,0:T(8,128)(2,1)S(1)} %get-tuple-element.86), channel_id=1, source_target_pairs={{0,1},{1,0},{2,3},{3,2},{4,5},{5,4},{6,7},{7,6},{8,9},{9,8},{10,11... | collective-permute-start | bytes 1769480 | tf_op jit(solution)/shard_map/cond/branch_1_fun/ppermute | solution.py:345
  4.3 11.2 %collective-permute-start.9 = (bf16[1,1,2,384,384]{4,3,2,1,0:T(8,128)(2,1)S(1)}, bf16[1,1,2,384,384]{4,3,2,1,0:T(8,128)(2,1)S(1)}, u32[]{:S(2)}, u32[]{:S(2)}) collective-permute-start(bf16[1,1,2,384,384]{4,3,2,1,0:T(8,128)(2,1)S(1)} %get-tuple-element.86), channel_id=1, source_target_pairs={{1,2},{2,1},{3,4},{4,3},{5,6},{6,5},{9,10},{10,9},{11,12},{12,11},... | collective-permute-start | bytes 1769480 | tf_op jit(solution)/shard_map/cond/branch_1_fun/ppermute | solution.py:345
  6.9 24.2 %collective-permute-start.12 = (bf16[624,768]{1,0:T(8,128)(2,1)S(1)}, bf16[624,768]{1,0:T(8,128)(2,1)S(1)}, u32[]{:S(2)}, u32[]{:S(2)}) collective-permute-start(bf16[624,768]{1,0:T(8,128)(2,1)S(1)} %get-tuple-element.89), channel_id=1, source_target_pairs={{0,8},{8,0},{16,24},{24,16},{32,40},{40,32},{48,56},{56,48},{64,72... | collective-permute-start | bytes 2875400 | tf_op jit(solution)/shard_map/cond/branch_1_fun/ppermute | solution.py:345
  7.8 29.3 %collective-permute-start.13 = (bf16[624,768]{1,0:T(8,128)(2,1)S(1)}, bf16[624,768]{1,0:T(8,128)(2,1)S(1)}, u32[]{:S(2)}, u32[]{:S(2)}) collective-permute-start(bf16[624,768]{1,0:T(8,128)(2,1)S(1)} %get-tuple-element.90), channel_id=1, source_target_pairs={{8,16},{16,8},{24,32},{32,24},{40,48},{48,40},{56,64},{64,56},{72,... | collective-permute-start | bytes 2875400 | tf_op jit(solution)/shard_map/cond/branch_1_fun/ppermute | solution.py:345
  19.0 20.5 %collective-permute-start.14 = (bf16[256,768]{1,0:T(8,128)(2,1)S(1)}, bf16[256,768]{1,0:T(8,128)(2,1)S(1)}, u32[]{:S(2)}, u32[]{:S(2)}) collective-permute-start(bf16[256,768]{1,0:T(8,128)(2,1)S(1)} %get-tuple-element.96.early), channel_id=1, source_target_pairs={{0,8},{8,0},{16,24},{24,16},{32,40},{40,32},{48,56},{56,48},{64,72... | collective-permute-start | bytes 1179656 | tf_op jit(solution)/shard_map/cond/branch_1_fun/ppermute | solution.py:345
  19.9 25.6 %collective-permute-start.15 = (bf16[256,768]{1,0:T(8,128)(2,1)S(1)}, bf16[256,768]{1,0:T(8,128)(2,1)S(1)}, u32[]{:S(2)}, u32[]{:S(2)}) collective-permute-start(bf16[256,768]{1,0:T(8,128)(2,1)S(1)} %get-tuple-element.96.early), channel_id=1, source_target_pairs={{8,16},{16,8},{24,32},{32,24},{40,48},{48,40},{56,64},{64,56},{72,... | collective-permute-start | bytes 1179656 | tf_op jit(solution)/shard_map/cond/branch_1_fun/ppermute | solution.py:345
  25.6 21.3 %collective-permute-start.10 = (bf16[128,768]{1,0:T(8,128)(2,1)S(1)}, bf16[128,768]{1,0:T(8,128)(2,1)S(1)}, u32[]{:S(2)}, u32[]{:S(2)}) collective-permute-start(bf16[128,768]{1,0:T(8,128)(2,1)S(1)} %get-tuple-element.87.late), channel_id=1, source_target_pairs={{0,8},{8,0},{16,24},{24,16},{32,40},{40,32},{48,56},{56,48},{64,72... | collective-permute-start | bytes 589832 | tf_op jit(solution)/shard_map/cond/branch_1_fun/ppermute | solution.py:345
  31.1 18.4 %collective-permute-start.11 = (bf16[128,768]{1,0:T(8,128)(2,1)S(1)}, bf16[128,768]{1,0:T(8,128)(2,1)S(1)}, u32[]{:S(2)}, u32[]{:S(2)}) collective-permute-start(bf16[128,768]{1,0:T(8,128)(2,1)S(1)} %get-tuple-element.87.late), channel_id=1, source_target_pairs={{8,16},{16,8},{24,32},{32,24},{40,48},{48,40},{56,64},{64,56},{72,... | collective-permute-start | bytes 589832 | tf_op jit(solution)/shard_map/cond/branch_1_fun/ppermute | solution.py:345
